TPU v7x, 256 devices: a whole 4x4x8 slice. The times are simulated.
256 devices in a mesh: gx: 32 (over x_lo, z, core), gy: 8 (over y, x_hi).
Axes of the slice: x: 4 (x_hi: 2, x_lo: 2; x = x_hi * 2 + x_lo), y: 4, z: 8, core: 2. Of those that a mesh axis runs over, the one named last changes fastest.
Arguments:
- adjoint: bfloat16 [512, 1024, 512], P('gx', 'gy'), may hold values from -6 to 6
- conduct_x: float32 [512, 1024], P('gx', 'gy'), may hold values from 0.02 to 0.24
- conduct_y: float32 [512, 1024], P('gx', 'gy'), may hold values from 0.02 to 0.24
- pick_weights: bfloat16 [512, 512, 1024], P(None, 'gx', 'gy'), may hold values from -0.015625 to 0.015625
- owner_order: int32 [512], replicated, may hold values from 0 to 511, each once
Outputs:
- smoothed: bfloat16 [512, 1024, 512], P('gx', 'gy')
- representer: float32 [512, 512], P(('gx', 'gy'))
Inputs may be any that keep to these rules, and one draw needn't show every extreme that they name: `owner_order`: each of 0 to 511 appears once.
All inputs are finite; a program needn't handle non-finite values.
Results may differ from a plain program's by a relative error of at most 0.0029.
Values may be sent and summed in bfloat16 or wider, within the bound.
No kernel may reach another device: no remote copies, remote signals or barrier semaphores. Data moves between devices by JAX's collectives and lax.ppermute only.
A program may use at most 64 MiB of HBM per device.

v0:
```python
import jax
import jax.numpy as jnp
from jax import lax
from jax.sharding import PartitionSpec as P

PANEL = 256
PANELS = 2
STEPS = 4


def extended(array, sides, width):
    for axis, dim in sides:
        peers, length = (lax.axis_size(axis), array.shape[dim])
        up = [(i, (i + 1) % peers) for i in range(peers - 1)]
        down = [(j, i) for i, j in up]
        last = lax.slice_in_dim(array, length - width, length, axis=dim)
        leading = lax.slice_in_dim(array, 0, width, axis=dim)
        before = lax.ppermute(last, axis, up)
        after = lax.ppermute(leading, axis, down)
        array = jnp.concatenate([before, array, after], axis=dim)
    return array


def in_blocks(array, dim, peers):
    before, after = (array.shape[:dim], array.shape[dim + 1 :])
    return jnp.moveaxis(array.reshape(*before, peers, -1, *after), dim, 0)


def summed_on_arrival(array, axis, dim):
    parts = in_blocks(array, dim, lax.axis_size(axis))
    arrived = lax.all_to_all(parts, axis, split_axis=0, concat_axis=0, tiled=True)
    return arrived.sum(axis=0)


def diffuse(field, conx, cony):
    centre = field[1:-1, 1:-1]
    above = field[:-2, 1:-1]
    below = field[2:, 1:-1]
    leftside = field[1:-1, :-2]
    rightside = field[1:-1, 2:]
    result = centre + conx[:-2, 1:-1, None] * (above - centre)
    result = result + conx[1:-1, 1:-1, None] * (below - centre)
    result = result + cony[1:-1, :-2, None] * (leftside - centre)
    result = result + cony[1:-1, 1:-1, None] * (rightside - centre)
    return result


def per_device(adjoint, conduct_x, conduct_y, pick_weights, owner_order):
    cells_x, cells_y, total_cols = adjoint.shape
    picks = pick_weights.shape[0]
    full_x = cells_x * lax.axis_size("gx")
    full_y = cells_y * lax.axis_size("gy")
    rows_idx = lax.axis_index("gx") * cells_x + jnp.arange(cells_x, dtype=jnp.int32)[:, None]
    cols_idx = lax.axis_index("gy") * cells_y + jnp.arange(cells_y, dtype=jnp.int32)[None, :]
    conx = jnp.where(rows_idx < full_x - 1, conduct_x, jnp.float32(0.0))
    cony = jnp.where(cols_idx < full_y - 1, conduct_y, jnp.float32(0.0))
    stacked = jnp.stack([conx, cony])
    coeff_wide = extended(stacked, (("gx", 1), ("gy", 2)), STEPS)
    sorted_weights = jnp.take(pick_weights.reshape(picks, cells_x * cells_y), owner_order, axis=0)
    smooth_list = []
    repr_list = []
    for panel in range(PANELS):
        block = adjoint[:, :, panel * PANEL : (panel + 1) * PANEL]
        field = extended(block, (("gx", 0), ("gy", 1)), STEPS).astype(jnp.float32)
        coeffs = coeff_wide
        for step in range(STEPS):
            field = diffuse(field, coeffs[0], coeffs[1])
            coeffs = coeffs[:, 1:-1, 1:-1]
        rounded = field.astype(jnp.bfloat16)
        smooth_list.append(rounded)
        flat_panel = rounded.reshape(cells_x * cells_y, PANEL)
        partial_value = jnp.dot(sorted_weights, flat_panel, preferred_element_type=jnp.float32)
        partial_value = partial_value.reshape(lax.axis_size("gx"), lax.axis_size("gy"), -1, PANEL)
        partial_value = summed_on_arrival(partial_value, "gy", 1)
        partial_value = summed_on_arrival(partial_value, "gx", 0)
        owned = partial_value.reshape(-1, PANEL)
        repr_list.append(owned)
    return (jnp.concatenate(smooth_list, axis=2), jnp.concatenate(repr_list, axis=1))


def solution(mesh):
    return jax.shard_map(
        per_device,
        mesh=mesh,
        in_specs=(P("gx", "gy", None), P("gx", "gy"), P("gx", "gy"), P(None, "gx", "gy"), P()),
        out_specs=(P("gx", "gy", None), P(("gx", "gy"), None)),
        check_vma=False,
    )
```

profile of v0, /device:TPU:1, one launch (start us, length us, event | category | flops | bytes accessed | tf_op | source)
XLA Modules:
  0.0 151.8 jit_solution(4381886208493955492)
XLA Ops:
  1.6 4.9 %collective-permute-start.4 = (f32[2,4,128]{2,1,0:T(4,128)S(1)}, f32[2,4,128]{2,1,0:T(4,128)S(1)}, u32[]{:S(2)}, u32[]{:S(2)}) collective-permute-start(f32[2,4,128]{2,1,0:T(4,128)S(1)} %get-tuple-element.46), channel_id=1, source_target_pairs={{0,8},{8,16},{16,24},{24,32},{32,40},{40,48},{48,56},{56,64},{64,7... | collective-permute-start | bytes 12296 | tf_op jit(solution)/shard_map/ppermute | solution.py:18
  8.5 2.1 %fusion.76 = (bf16[4,128,256]{2,1,0:T(8,128)(2,1)S(1)}, bf16[4,128,256]{2,1,0:T(8,128)(2,1)}, bf16[4,128,256]{2,1,0:T(8,128)(2,1)S(1)}, bf16[4,128,256]{2,1,0:T(8,128)(2,1)}) fusion(bf16[16,128,512]{2,1,0:T(8,128)(2,1)} %param.5), kind=kLoop, calls=%fused_computation.136 | loop fusion | bytes 2097152 | tf_op jit(solution)/shard_map/slice | solution.py:16
  10.6 3.6 %collective-permute-start.8 = (bf16[4,128,256]{2,1,0:T(8,128)(2,1)}, bf16[4,128,256]{2,1,0:T(8,128)(2,1)S(1)}, u32[]{:S(2)}, u32[]{:S(2)}) collective-permute-start(bf16[4,128,256]{2,1,0:T(8,128)(2,1)} %get-tuple-element.3), channel_id=1, source_target_pairs={{0,8},{8,16},{16,24},{24,32},{32,40},{40,48},{48,56},{56,64},{64,7... | collective-permute-start | bytes 786440 | tf_op jit(solution)/shard_map/ppermute | solution.py:18
  16.1 3.6 %collective-permute-start = (bf16[4,128,256]{2,1,0:T(8,128)(2,1)S(1)}, bf16[4,128,256]{2,1,0:T(8,128)(2,1)S(1)}, u32[]{:S(2)}, u32[]{:S(2)}) collective-permute-start(bf16[4,128,256]{2,1,0:T(8,128)(2,1)S(1)} %get-tuple-element.2), channel_id=1, source_target_pairs={{0,8},{8,16},{16,24},{24,32},{32,40},{40,48},{48,56},{56,64},{64,7... | collective-permute-start | bytes 786440 | tf_op jit(solution)/shard_map/ppermute | solution.py:18
  21.7 3.3 %gather_fusion = bf16[512,2048]{1,0:T(8,128)(2,1)} fusion(bf16[512,2048]{1,0:T(8,128)(2,1)S(1)} %bitcast.46, s32[1024]{0:T(1024)S(1)} %pad_clamp_fusion), kind=kCustom, calls=%fused_computation | custom fusion | bytes 4196352 | tf_op jit(solution)/shard_map/jit(_take)/gather | solution.py:59
  25.0 3.3 %broadcast_select_fusion = bf16[512,2048]{1,0:T(8,128)(2,1)} fusion(bf16[512,2048]{1,0:T(8,128)(2,1)} %gather_fusion, pred[512]{0:T(512)(128)(4,1)S(1)} %compare_and_fusion), kind=kLoop, calls=%fused_computation.101 | loop fusion | flops 1048576 | bytes 4194816 | tf_op jit(solution)/shard_map/jit(_take)/select_n | solution.py:59
  28.4 4.6 %collective-permute-start.6 = (f32[2,24,4]{2,1,0:T(8,128)S(1)}, f32[2,24,4]{2,1,0:T(8,128)S(1)}, u32[]{:S(2)}, u32[]{:S(2)}) collective-permute-start(f32[2,24,4]{2,1,0:T(8,128)S(1)} %get-tuple-element.44), channel_id=1, source_target_pairs={{0,1},{1,2},{2,3},{3,4},{4,5},{5,6},{6,7},{8,9},{9,10},{10,11},{11... | collective-permute-start | bytes 2312 | tf_op jit(solution)/shard_map/ppermute | solution.py:18
  34.6 4.4 %select_n.40 = bf16[32,8,2,2048]{3,2,1,0:T(2,128)(2,1)} reshape(bf16[512,2048]{1,0:T(8,128)(2,1)} %broadcast_select_fusion) | data formatting | bytes 4194304 | tf_op jit(solution)/shard_map/jit(_take)/select_n | solution.py:59
  45.1 5.5 %collective-permute-start.10 = (bf16[24,4,256]{2,1,0:T(4,128)(2,1)S(1)}, bf16[24,4,256]{2,1,0:T(4,128)(2,1)S(1)}, u32[]{:S(2)}, u32[]{:S(2)}) collective-permute-start(bf16[24,4,256]{2,1,0:T(4,128)(2,1)S(1)} %get-tuple-element.10), channel_id=1, source_target_pairs={{0,1},{1,2},{2,3},{3,4},{4,5},{5,6},{6,7},{8,9},{9,10},{10,11},{11... | collective-permute-start | bytes 147464 | tf_op jit(solution)/shard_map/ppermute | solution.py:18
  51.9 5.5 %collective-permute-start.2 = (bf16[24,4,256]{2,1,0:T(4,128)(2,1)S(1)}, bf16[24,4,256]{2,1,0:T(4,128)(2,1)S(1)}, u32[]{:S(2)}, u32[]{:S(2)}) collective-permute-start(bf16[24,4,256]{2,1,0:T(4,128)(2,1)S(1)} %get-tuple-element.8), channel_id=1, source_target_pairs={{0,1},{1,2},{2,3},{3,4},{4,5},{5,6},{6,7},{8,9},{9,10},{10,11},{11... | collective-permute-start | bytes 147464 | tf_op jit(solution)/shard_map/ppermute | solution.py:18
  59.3 5.2 %collective-permute-done.3 = bf16[24,4,256]{2,1,0:T(4,128)(2,1)S(1)} collective-permute-done((bf16[24,4,256]{2,1,0:T(4,128)(2,1)S(1)}, bf16[24,4,256]{2,1,0:T(4,128)(2,1)S(1)}, u32[]{:S(2)}, u32[]{:S(2)}) %collective-permute-start.3) | collective-permute-done | bytes 49184 | tf_op jit(solution)/shard_map/ppermute | solution.py:19
  65.1 5.2 %fusion.9 = (f32[22,134,256]{2,1,0:T(8,128)S(1)}, f32[22,134,256]{2,1,0:T(8,128)S(1)}) fusion(f32[24,136,256]{2,1,0:T(8,128)S(1)} %maximum_convert_fusion, f32[22,134]{1,0:T(8,128)S(1)} %copy-done.8, f32[22,134]{1,0:T(8,128)S(1)} %copy-done.7, f32[22,134]{1,0:T(8,128)S(1)} %copy-done.6, f32[22,134]{1,0:T(8,128)S(1)} %copy-done.5, ...), kind=kLoop, calls=%fused_computation.15 | loop fusion | flops 18112512 | bytes 36272192 | tf_op jit(solution)/shard_map/add | solution.py:44
  70.3 4.4 %fusion.25 = (f32[20,132,256]{2,1,0:T(8,128)S(1)}, f32[20,132,256]{2,1,0:T(8,128)S(1)}) fusion(f32[22,134,256]{2,1,0:T(8,128)S(1)} %get-tuple-element.16, f32[20,132]{1,0:T(8,128)S(1)} %copy-done.4, f32[20,132]{1,0:T(8,128)S(1)} %copy-done.3, f32[20,132]{1,0:T(8,128)S(1)} %get-tuple-element.37, f32[20,132]{1,0:T(8,128)S(1)} %get-tuple-element.36, ...), kind=kLoop, calls=%fused_computation.39 | loop fusion | flops 16220160 | bytes 32482560 | tf_op jit(solution)/shard_map/add | solution.py:44
  74.8 3.8 %fusion.41 = (f32[18,130,256]{2,1,0:T(8,128)S(1)}, f32[18,130,256]{2,1,0:T(8,128)S(1)}) fusion(f32[20,132,256]{2,1,0:T(8,128)S(1)} %get-tuple-element.14, f32[18,130]{1,0:T(8,128)S(1)} %get-tuple-element.35, f32[18,130]{1,0:T(8,128)S(1)} %get-tuple-element.34, f32[18,130]{1,0:T(8,128)S(1)} %get-tuple-element.33, f32[18,130]{1,0:T(8,128)S(1)} %get-tuple-element.32, ...), kind=kLoop, calls=%fused_computation.63 | loop fusion | flops 14376960 | bytes 28791360 | tf_op jit(solution)/shard_map/add | solution.py:44
  78.7 3.4 %fusion.59 = (bf16[16,128,256]{2,1,0:T(8,128)(2,1)S(1)}, bf16[16,128,256]{2,1,0:T(8,128)(2,1)S(1)}) fusion(f32[18,130,256]{2,1,0:T(8,128)S(1)} %get-tuple-element.12, f32[16,128]{1,0:T(8,128)S(1)} %copy-done.12, f32[16,128]{1,0:T(8,128)S(1)} %copy-done.11, f32[16,128]{1,0:T(8,128)S(1)} %copy-done.10, f32[16,128]{1,0:T(8,128)S(1)} %copy-done.9, ...), kind=kLoop, calls=%fused_computation.90 | loop fusion | flops 13631488 | bytes 23101440 | tf_op jit(solution)/shard_map/convert_element_type | solution.py:69
  83.9 7.6 %all-to-all-start = ((f32[8,32,1,2,256]{4,3,1,2,0:T(2,128)}), f32[8,32,1,2,256]{4,3,1,2,0:T(2,128)S(1)}, u32[]{:S(2)}, u32[]{:S(2)}) async-start(f32[8,32,1,2,256]{4,3,1,2,0:T(2,128)} %copy.10), calls=%async_computation | async-start | bytes 1048576 | tf_op jit(solution)/shard_map/all_to_all | solution.py:31
  91.5 2.3 %fusion.73 = f32[8,32,1,2,256]{4,0,3,1,2:T(8,128)S(1)} fusion(bf16[2048,256,1,1]{1,0,3,2:T(8,128)(2,1)S(1)} %bitcast.48, bf16[32,8,2,2048]{3,2,1,0:T(2,128)(2,1)} %select_n.40), kind=kOutput, calls=%fused_computation.109 | convolution fusion | flops 536870912 | bytes 3670016 | tf_op jit(solution)/shard_map/dot_general | solution.py:72
  94.9 7.4 %all-to-all-done = f32[8,32,1,2,256]{4,3,1,2,0:T(2,128)S(1)} async-done(((f32[8,32,1,2,256]{4,3,1,2,0:T(2,128)}), f32[8,32,1,2,256]{4,3,1,2,0:T(2,128)S(1)}, u32[]{:S(2)}, u32[]{:S(2)}) %all-to-all-start) | async-done | bytes 524320 | tf_op jit(solution)/shard_map/all_to_all | solution.py:31
  102.3 3.5 %all-to-all-start.2 = ((f32[8,32,1,2,256]{4,3,1,2,0:T(2,128)}), f32[8,32,1,2,256]{4,3,1,2,0:T(2,128)S(1)}, u32[]{:S(2)}, u32[]{:S(2)}) async-start(f32[8,32,1,2,256]{4,3,1,2,0:T(2,128)} %copy.12), calls=%async_computation.2 | async-start | bytes 1048576 | tf_op jit(solution)/shard_map/all_to_all | solution.py:31
  106.6 8.7 %all-to-all-done.2 = f32[8,32,1,2,256]{4,3,1,2,0:T(2,128)S(1)} async-done(((f32[8,32,1,2,256]{4,3,1,2,0:T(2,128)}), f32[8,32,1,2,256]{4,3,1,2,0:T(2,128)S(1)}, u32[]{:S(2)}, u32[]{:S(2)}) %all-to-all-start.2) | async-done | bytes 524320 | tf_op jit(solution)/shard_map/all_to_all | solution.py:31
  115.3 14.8 %all-to-all-start.1 = ((f32[32,1,1,2,256]{4,3,2,1,0:T(2,128)}), f32[32,1,1,2,256]{4,3,2,1,0:T(2,128)S(1)}, u32[]{:S(2)}, u32[]{:S(2)}) async-start(f32[32,1,1,2,256]{4,3,2,1,0:T(2,128)} %bitcast.15), calls=%async_computation.1 | async-start | bytes 131072 | tf_op jit(solution)/shard_map/all_to_all | solution.py:31
  131.0 7.3 %all-to-all-done.1 = f32[32,1,1,2,256]{4,3,2,1,0:T(2,128)S(1)} async-done(((f32[32,1,1,2,256]{4,3,2,1,0:T(2,128)}), f32[32,1,1,2,256]{4,3,2,1,0:T(2,128)S(1)}, u32[]{:S(2)}, u32[]{:S(2)}) %all-to-all-start.1) | async-done | bytes 65568 | tf_op jit(solution)/shard_map/all_to_all | solution.py:31
  138.3 4.7 %all-to-all-start.3 = ((f32[32,1,1,2,256]{4,3,2,1,0:T(2,128)}), f32[32,1,1,2,256]{4,3,2,1,0:T(2,128)S(1)}, u32[]{:S(2)}, u32[]{:S(2)}) async-start(f32[32,1,1,2,256]{4,3,2,1,0:T(2,128)} %bitcast.21), calls=%async_computation.3 | async-start | bytes 131072 | tf_op jit(solution)/shard_map/all_to_all | solution.py:31
  144.5 6.6 %all-to-all-done.3 = f32[32,1,1,2,256]{4,3,2,1,0:T(2,128)S(1)} async-done(((f32[32,1,1,2,256]{4,3,2,1,0:T(2,128)}), f32[32,1,1,2,256]{4,3,2,1,0:T(2,128)S(1)}, u32[]{:S(2)}, u32[]{:S(2)}) %all-to-all-start.3) | async-done | bytes 65568 | tf_op jit(solution)/shard_map/all_to_all | solution.py:31
  (80 shorter events, 24.8 us)
Async XLA Ops:
  0.7 20.5 %copy-start.1 = (bf16[512,16,128]{2,1,0:T(8,128)(2,1)S(1)}, bf16[512,16,128]{2,1,0:T(8,128)(2,1)}, u32[]{:S(2)}) copy-start(bf16[512,16,128]{2,1,0:T(8,128)(2,1)} %param.8) | copy-start | bytes 6291460
  1.6 26.7 %collective-permute-start.4 = (f32[2,4,128]{2,1,0:T(4,128)S(1)}, f32[2,4,128]{2,1,0:T(4,128)S(1)}, u32[]{:S(2)}, u32[]{:S(2)}) collective-permute-start(f32[2,4,128]{2,1,0:T(4,128)S(1)} %get-tuple-element.46), channel_id=1, source_target_pairs={{0,8},{8,16},{16,24},{24,32},{32,40},{40,48},{48,56},{56,64},{64,7... | collective-permute-start | bytes 12296 | tf_op jit(solution)/shard_map/ppermute | solution.py:18
  6.6 21.8 %collective-permute-start.5 = (f32[2,4,128]{2,1,0:T(4,128)S(1)}, f32[2,4,128]{2,1,0:T(4,128)S(1)}, u32[]{:S(2)}, u32[]{:S(2)}) collective-permute-start(f32[2,4,128]{2,1,0:T(4,128)S(1)} %get-tuple-element.47), channel_id=1, source_target_pairs={{8,0},{16,8},{24,16},{32,24},{40,32},{48,40},{56,48},{64,56},{72,6... | collective-permute-start | bytes 12296 | tf_op jit(solution)/shard_map/ppermute | solution.py:19
  10.6 34.4 %collective-permute-start.8 = (bf16[4,128,256]{2,1,0:T(8,128)(2,1)}, bf16[4,128,256]{2,1,0:T(8,128)(2,1)S(1)}, u32[]{:S(2)}, u32[]{:S(2)}) collective-permute-start(bf16[4,128,256]{2,1,0:T(8,128)(2,1)} %get-tuple-element.3), channel_id=1, source_target_pairs={{0,8},{8,16},{16,24},{24,32},{32,40},{40,48},{48,56},{56,64},{64,7... | collective-permute-start | bytes 786440 | tf_op jit(solution)/shard_map/ppermute | solution.py:18
  14.2 30.8 %collective-permute-start.9 = (bf16[4,128,256]{2,1,0:T(8,128)(2,1)}, bf16[4,128,256]{2,1,0:T(8,128)(2,1)S(1)}, u32[]{:S(2)}, u32[]{:S(2)}) collective-permute-start(bf16[4,128,256]{2,1,0:T(8,128)(2,1)} %get-tuple-element.5), channel_id=1, source_target_pairs={{8,0},{16,8},{24,16},{32,24},{40,32},{48,40},{56,48},{64,56},{72,6... | collective-permute-start | bytes 786440 | tf_op jit(solution)/shard_map/ppermute | solution.py:19
  16.1 35.7 %collective-permute-start = (bf16[4,128,256]{2,1,0:T(8,128)(2,1)S(1)}, bf16[4,128,256]{2,1,0:T(8,128)(2,1)S(1)}, u32[]{:S(2)}, u32[]{:S(2)}) collective-permute-start(bf16[4,128,256]{2,1,0:T(8,128)(2,1)S(1)} %get-tuple-element.2), channel_id=1, source_target_pairs={{0,8},{8,16},{16,24},{24,32},{32,40},{40,48},{48,56},{56,64},{64,7... | collective-permute-start | bytes 786440 | tf_op jit(solution)/shard_map/ppermute | solution.py:18
  25.0 9.4 %copy-start = (bf16[16,128,512]{2,1,0:T(8,128)(2,1)S(1)}, bf16[16,128,512]{2,1,0:T(8,128)(2,1)}, u32[]{:S(2)}) copy-start(bf16[16,128,512]{2,1,0:T(8,128)(2,1)} %param.5) | copy-start | bytes 6291460
  28.4 10.6 %collective-permute-start.6 = (f32[2,24,4]{2,1,0:T(8,128)S(1)}, f32[2,24,4]{2,1,0:T(8,128)S(1)}, u32[]{:S(2)}, u32[]{:S(2)}) collective-permute-start(f32[2,24,4]{2,1,0:T(8,128)S(1)} %get-tuple-element.44), channel_id=1, source_target_pairs={{0,1},{1,2},{2,3},{3,4},{4,5},{5,6},{6,7},{8,9},{9,10},{10,11},{11... | collective-permute-start | bytes 2312 | tf_op jit(solution)/shard_map/ppermute | solution.py:18
  33.1 7.9 %collective-permute-start.7 = (f32[2,24,4]{2,1,0:T(8,128)S(1)}, f32[2,24,4]{2,1,0:T(8,128)S(1)}, u32[]{:S(2)}, u32[]{:S(2)}) collective-permute-start(f32[2,24,4]{2,1,0:T(8,128)S(1)} %get-tuple-element.45), channel_id=1, source_target_pairs={{1,0},{2,1},{3,2},{4,3},{5,4},{6,5},{7,6},{9,8},{10,9},{11,10},{12... | collective-permute-start | bytes 2312 | tf_op jit(solution)/shard_map/ppermute | solution.py:19
  39.1 12.8 %collective-permute-start.1 = (bf16[4,128,256]{2,1,0:T(8,128)(2,1)S(1)}, bf16[4,128,256]{2,1,0:T(8,128)(2,1)S(1)}, u32[]{:S(2)}, u32[]{:S(2)}) collective-permute-start(bf16[4,128,256]{2,1,0:T(8,128)(2,1)S(1)} %get-tuple-element.4), channel_id=1, source_target_pairs={{8,0},{16,8},{24,16},{32,24},{40,32},{48,40},{56,48},{64,56},{72,6... | collective-permute-start | bytes 786440 | tf_op jit(solution)/shard_map/ppermute | solution.py:19
  45.1 13.7 %collective-permute-start.10 = (bf16[24,4,256]{2,1,0:T(4,128)(2,1)S(1)}, bf16[24,4,256]{2,1,0:T(4,128)(2,1)S(1)}, u32[]{:S(2)}, u32[]{:S(2)}) collective-permute-start(bf16[24,4,256]{2,1,0:T(4,128)(2,1)S(1)} %get-tuple-element.10), channel_id=1, source_target_pairs={{0,1},{1,2},{2,3},{3,4},{4,5},{5,6},{6,7},{8,9},{9,10},{10,11},{11... | collective-permute-start | bytes 147464 | tf_op jit(solution)/shard_map/ppermute | solution.py:18
  50.6 8.2 %collective-permute-start.11 = (bf16[24,4,256]{2,1,0:T(4,128)(2,1)S(1)}, bf16[24,4,256]{2,1,0:T(4,128)(2,1)S(1)}, u32[]{:S(2)}, u32[]{:S(2)}) collective-permute-start(bf16[24,4,256]{2,1,0:T(4,128)(2,1)S(1)} %get-tuple-element.11), channel_id=1, source_target_pairs={{1,0},{2,1},{3,2},{4,3},{5,4},{6,5},{7,6},{9,8},{10,9},{11,10},{12... | collective-permute-start | bytes 147464 | tf_op jit(solution)/shard_map/ppermute | solution.py:19
  51.9 7.4 %collective-permute-start.2 = (bf16[24,4,256]{2,1,0:T(4,128)(2,1)S(1)}, bf16[24,4,256]{2,1,0:T(4,128)(2,1)S(1)}, u32[]{:S(2)}, u32[]{:S(2)}) collective-permute-start(bf16[24,4,256]{2,1,0:T(4,128)(2,1)S(1)} %get-tuple-element.8), channel_id=1, source_target_pairs={{0,1},{1,2},{2,3},{3,4},{4,5},{5,6},{6,7},{8,9},{9,10},{10,11},{11... | collective-permute-start | bytes 147464 | tf_op jit(solution)/shard_map/ppermute | solution.py:18
  57.4 7.1 %collective-permute-start.3 = (bf16[24,4,256]{2,1,0:T(4,128)(2,1)S(1)}, bf16[24,4,256]{2,1,0:T(4,128)(2,1)S(1)}, u32[]{:S(2)}, u32[]{:S(2)}) collective-permute-start(bf16[24,4,256]{2,1,0:T(4,128)(2,1)S(1)} %get-tuple-element.9), channel_id=1, source_target_pairs={{1,0},{2,1},{3,2},{4,3},{5,4},{6,5},{7,6},{9,8},{10,9},{11,10},{12... | collective-permute-start | bytes 147464 | tf_op jit(solution)/shard_map/ppermute | solution.py:19
  59.3 5.8 %copy-start.5 = (f32[22,134]{1,0:T(8,128)S(1)}, f32[22,134]{1,0:T(8,128)}, u32[]{:S(2)}) copy-start(f32[22,134]{1,0:T(8,128)} %get-tuple-element.40) | copy-start | bytes 35380
  59.3 5.8 %copy-start.6 = (f32[22,134]{1,0:T(8,128)S(1)}, f32[22,134]{1,0:T(8,128)}, u32[]{:S(2)}) copy-start(f32[22,134]{1,0:T(8,128)} %get-tuple-element.41) | copy-start | bytes 35380
  59.3 5.8 %copy-start.7 = (f32[22,134]{1,0:T(8,128)S(1)}, f32[22,134]{1,0:T(8,128)}, u32[]{:S(2)}) copy-start(f32[22,134]{1,0:T(8,128)} %get-tuple-element.42) | copy-start | bytes 35380
  59.3 5.8 %copy-start.8 = (f32[22,134]{1,0:T(8,128)S(1)}, f32[22,134]{1,0:T(8,128)}, u32[]{:S(2)}) copy-start(f32[22,134]{1,0:T(8,128)} %get-tuple-element.43) | copy-start | bytes 35380
  65.1 5.2 %copy-start.3 = (f32[20,132]{1,0:T(8,128)S(1)}, f32[20,132]{1,0:T(8,128)}, u32[]{:S(2)}) copy-start(f32[20,132]{1,0:T(8,128)} %get-tuple-element.38) | copy-start | bytes 31684
  65.1 5.2 %copy-start.4 = (f32[20,132]{1,0:T(8,128)S(1)}, f32[20,132]{1,0:T(8,128)}, u32[]{:S(2)}) copy-start(f32[20,132]{1,0:T(8,128)} %get-tuple-element.39) | copy-start | bytes 31684
  83.9 18.4 %all-to-all-start = ((f32[8,32,1,2,256]{4,3,1,2,0:T(2,128)}), f32[8,32,1,2,256]{4,3,1,2,0:T(2,128)S(1)}, u32[]{:S(2)}, u32[]{:S(2)}) async-start(f32[8,32,1,2,256]{4,3,1,2,0:T(2,128)} %copy.10), calls=%async_computation | async-start | bytes 1048576 | tf_op jit(solution)/shard_map/all_to_all | solution.py:31
  102.3 13.1 %all-to-all-start.2 = ((f32[8,32,1,2,256]{4,3,1,2,0:T(2,128)}), f32[8,32,1,2,256]{4,3,1,2,0:T(2,128)S(1)}, u32[]{:S(2)}, u32[]{:S(2)}) async-start(f32[8,32,1,2,256]{4,3,1,2,0:T(2,128)} %copy.12), calls=%async_computation.2 | async-start | bytes 1048576 | tf_op jit(solution)/shard_map/all_to_all | solution.py:31
  115.3 22.9 %all-to-all-start.1 = ((f32[32,1,1,2,256]{4,3,2,1,0:T(2,128)}), f32[32,1,1,2,256]{4,3,2,1,0:T(2,128)S(1)}, u32[]{:S(2)}, u32[]{:S(2)}) async-start(f32[32,1,1,2,256]{4,3,2,1,0:T(2,128)} %bitcast.15), calls=%async_computation.1 | async-start | bytes 131072 | tf_op jit(solution)/shard_map/all_to_all | solution.py:31
  138.3 12.9 %all-to-all-start.3 = ((f32[32,1,1,2,256]{4,3,2,1,0:T(2,128)}), f32[32,1,1,2,256]{4,3,2,1,0:T(2,128)S(1)}, u32[]{:S(2)}, u32[]{:S(2)}) async-start(f32[32,1,1,2,256]{4,3,2,1,0:T(2,128)} %bitcast.21), calls=%async_computation.3 | async-start | bytes 131072 | tf_op jit(solution)/shard_map/all_to_all | solution.py:31
  (5 other events, 18.9 us)
where the time goes:
time: 153 us; the launch traced here: 152 us
  starting transfers between devices  68.1 us (45%)
  waiting for transfers between devices  35.2 us (23%)
  other arithmetic  27.5 us (18%)
  local copies, waits for them, and re-layouts  16.8 us (11%)
  matrix products  3.09 us (2%)
    all_to_all x4, starting transfers between devices, summed_on_arrival(): lax.all_to_all(parts, axis, split_axis=0, concat_axis=0, tiled=True)  30.7 us
    all_to_all x4, waiting for transfers between devices, summed_on_arrival(): lax.all_to_all(parts, axis, split_axis=0, concat_axis=0, tiled=True)  30 us
    ppermute x6, starting transfers between devices, extended(): before = lax.ppermute(last, axis, up)  27.8 us
    add x3, other arithmetic, diffuse(): result = result + cony[1:-1, 1:-1, None] * (rightside - centre)  13.5 us
    ppermute x6, starting transfers between devices, extended(): after = lax.ppermute(leading, axis, down)  9.63 us
    ppermute x6, waiting for transfers between devices, extended(): after = lax.ppermute(leading, axis, down)  5.19 us
    select_n x1, local copies, waits for them, and re-layouts, per_device(): jnp.take(pick_weights.reshape(picks, cells_x * cells_y), owner_order, axi...  4.41 us
    select_n x2, other arithmetic, per_device(): jnp.take(pick_weights.reshape(picks, cells_x * cells_y), owner_order, axi...  4 us
  transfers between devices with their start and end apart: 16, of which 5 were waited for; matrix products, arithmetic and copies ran while one was open for 17% of the time, Pallas kernels for 0%

commit v1 on v0

v1 whole, which is shorter than its diff:
```python
import jax
import jax.numpy as jnp
from jax import lax
from jax.experimental import pallas as pl
from jax.experimental.pallas import tpu as pltpu
from jax.sharding import Mesh
from jax.sharding import PartitionSpec as P

STEPS = 4
BF = jnp.bfloat16
F32 = jnp.float32
VMEM = pl.BlockSpec(memory_space=pltpu.VMEM)
SMEM = pl.BlockSpec(memory_space=pltpu.SMEM)
HBM = pl.BlockSpec(memory_space=pltpu.HBM)
MIB = 1024 * 1024
ALONG = ("g", "core")
PITCH = 520


def parity_x():
    return lax.axis_index("core")


def parity_y():
    return lax.rem(lax.axis_index("gy"), 2)


def split_pair(value):
    high = value.astype(BF)
    return high, (value - high.astype(F32)).astype(BF)


def low_sublanes(shape):
    return lax.broadcasted_iota(jnp.int32, shape, 0) < 4


def pack_columns(adj, kx, ky, even, odd, pair, full, first, last, kxv, kyv, sems):
    cells_x, cells_y, _ = adj.shape
    coefs = [
        pltpu.make_async_copy(kx, kxv, sems.at[2]),
        pltpu.make_async_copy(ky, kyv, sems.at[3]),
    ]
    strips = [
        pltpu.make_async_copy(adj.at[:, pl.ds(0, 8)], first, sems.at[0]),
        pltpu.make_async_copy(adj.at[:, pl.ds(cells_y - 8, 8)], last, sems.at[1]),
    ]
    for copy in coefs + strips:
        copy.start()
    is_last_x = jnp.logical_and(
        lax.axis_index("g") == lax.axis_size("g") - 1, parity_x() == 1
    )
    is_last_y = lax.axis_index("gy") == lax.axis_size("gy") - 1
    end_x = jnp.where(is_last_x, cells_x - 1, -1)
    end_y = jnp.where(is_last_y, cells_y - 1, -1)
    row = lax.broadcasted_iota(jnp.int32, (cells_x, cells_y), 0)
    col = lax.broadcasted_iota(jnp.int32, (cells_x, cells_y), 1)
    for copy in coefs:
        copy.wait()
    conx = jnp.where(row == end_x, 0.0, kxv[...])
    cony = jnp.where(col == end_y, 0.0, kyv[...])
    full[:, :cells_y] = conx
    full[:, cells_y:] = cony
    pieces = jnp.concatenate([*split_pair(conx), *split_pair(cony)], axis=1)
    pair[...] = pieces
    even[64:80, :] = pieces
    odd[64:80, :] = pieces
    for copy in strips:
        copy.wait()
    is_even = parity_y() == 0
    for i in range(8):
        a, b = first[i].astype(F32), first[i + 8].astype(F32)
        c, d = last[i].astype(F32), last[i + 8].astype(F32)
        low = low_sublanes(a.shape)
        leftward = jnp.where(low, a, pltpu.roll(b, 4, 0))
        rightward = jnp.where(low, pltpu.roll(c, 4, 0), d)
        even[8 * i : 8 * i + 8, :] = jnp.where(is_even, rightward, leftward).astype(BF)
        odd[8 * i : 8 * i + 8, :] = jnp.where(is_even, leftward, rightward).astype(BF)


def side_bases(cells_x):
    is_even = parity_x() == 0
    return jnp.where(is_even, cells_x - 4, 0), jnp.where(is_even, 0, cells_x - 4)


def order_weights(order, weights, out, ready, spread):
    picks, cells_x, cells_y = weights.shape
    core = parity_x()
    ready[...] = jnp.zeros_like(ready)

    @pl.loop(0, picks // 32)
    def _(g):
        for c in range(2):
            base = jnp.bitwise_xor(core, c) * (picks // 2) + g * 16
            for s in range(16):
                pick = order[g * 32 + c * 16 + s]
                spread[pl.ds(base + s, cells_x, stride=PITCH), :] = weights[pick].astype(F32)

    @pl.loop(0, cells_x)
    def _(i):
        block = spread[pl.ds(pl.multiple_of(i * PITCH, 8), picks), :]
        out[:, pl.ds(pl.multiple_of(i * cells_y, cells_y), cells_y)] = block.astype(BF)


def pack_rows(adj, pair, y_even, y_odd, ready, even, odd, halo, kh, sems):
    cells_x, cells_y, _ = adj.shape
    del ready
    is_even = parity_x() == 0
    base_even, base_odd = side_bases(cells_x)
    copies = []
    for k in range(4):
        for n, (base, out) in enumerate(((base_even, even), (base_odd, odd))):
            copies.append(
                pltpu.make_async_copy(
                    adj.at[base + k], out.at[pl.ds(k * cells_y, cells_y)], sems.at[2 * k + n]
                )
            )
    for copy in copies:
        copy.start()
    y_is_even = parity_y() == 0
    for i in range(8):
        e, o = y_even[8 * i : 8 * i + 8, :].astype(F32), y_odd[8 * i : 8 * i + 8, :].astype(F32)
        right, left = jnp.where(y_is_even, e, o), jnp.where(y_is_even, o, e)
        low = low_sublanes(e.shape)
        halo[i] = jnp.where(low, right, pltpu.roll(left, 4, 0)).astype(BF)
        halo[i + 8] = jnp.where(low, pltpu.roll(right, 4, 0), left).astype(BF)
    e, o = y_even[64:80, :].astype(F32), y_odd[64:80, :].astype(F32)
    right, left = jnp.where(y_is_even, e, o), jnp.where(y_is_even, o, e)
    lane = lax.broadcasted_iota(jnp.int32, (cells_x, 128), 1)
    parts = []
    for n in range(4):
        span = slice(128 * n, 128 * n + 128)
        parts.append(jnp.where(lane < 4, right[:, span], pltpu.roll(left[:, span], 8, 1)))
    kh[:, :128] = parts[0] + parts[1]
    kh[:, 128:] = parts[2] + parts[3]
    side = jnp.concatenate(parts, axis=1)
    own = pair[...].astype(F32)
    tail = 4 * cells_y + 32
    for base, out, flag in ((base_even, even, is_even), (base_odd, odd, jnp.logical_not(is_even))):
        for k in range(4):
            out[4 * cells_y + 8 * k : 4 * cells_y + 8 * k + 8, :] = halo[base + k]
        out[tail : tail + 8, :] = jnp.where(flag, own[8:], own[:8]).astype(BF)
        out[tail + 8 : tail + 16, :] = jnp.where(flag, side[8:], side[:8]).astype(BF)
    for copy in copies:
        copy.wait()


def put(dst, r, own, side):
    lanes, _, depth, _ = dst.shape
    wrap = depth - 8
    for n in range(lanes):
        span = slice(128 * n, 128 * n + 128)
        dst[n, r, 8 : wrap - 8, :] = own[:, span]
        dst[n, r, wrap - 8 : wrap, :] = side[:, span]
        dst[n, r, 0:8, :] = side[:, span]
        dst[n, r, wrap : wrap + 8, :] = own[:8, span]


def put_coef(dst, r, own, side):
    a = jnp.broadcast_to(own, (own.shape[0], 128))
    b = jnp.broadcast_to(side, (8, 128))
    wrap = dst.shape[1] - 8
    dst[r, 8 : wrap - 8, :] = a
    dst[r, wrap - 8 : wrap, :] = b
    dst[r, 0:8, :] = b


def coefs_at(get_rest, get_up, get_down, get_y, q):
    s = pl.ds(8 + 8 * q, 8)
    (a, i), (b, j), (c, k), (d, m) = get_rest, get_up, get_down, get_y
    return a[i, s, :], b[j, s, :], c[k, s, :], d[m, s, :], d[m, pl.ds(7 + 8 * q, 8), :]


def cell(above, mid, below, q, n, coefs):
    rest, up, down, right, left = coefs
    p = 8 + 8 * q
    (a, i), (b, j), (c, k) = above, mid, below
    total = rest * b[n, j, pl.ds(p, 8), :] + up * a[n, i, pl.ds(p, 8), :]
    total = total + down * c[n, k, pl.ds(p, 8), :]
    total = total + right * b[n, j, pl.ds(p + 1, 8), :]
    return total + left * b[n, j, pl.ds(p - 1, 8), :]


def store(dst, r, q, n, tiles, value):
    dst[n, r, pl.ds(8 + 8 * q, 8), :] = value
    if q == 0:
        dst[n, r, pl.ds(8 + 8 * tiles, 8), :] = value
    if q == tiles - 1:
        dst[n, r, pl.ds(0, 8), :] = value


def rest_of(dst, row, edge_up, edge_down, cond_y, tiles):
    for q in range(tiles):
        _, up, down, right, left = coefs_at((dst, row), edge_up, edge_down, cond_y, q)
        dst[row, pl.ds(8 + 8 * q, 8), :] = 1.0 - (up + down + right + left)


def step_row(above, mid, below, coef_refs, dst, r, tiles, lanes):
    for q in range(tiles):
        coefs = coefs_at(*coef_refs, q)
        for n in range(lanes):
            store(dst, r, q, n, tiles, cell(above, mid, below, q, n, coefs))


def last_row(above, mid, below, coef_refs, out, r, tiles, lanes):
    for q in range(0, tiles - 1, 2):
        ca, cb = coefs_at(*coef_refs, q), coefs_at(*coef_refs, q + 1)
        for n in range(lanes):
            pair = [cell(above, mid, below, q, n, ca), cell(above, mid, below, q + 1, n, cb)]
            new = jnp.concatenate(pair, axis=0).astype(BF)
            out[r, pl.ds(8 * q, 16), pl.ds(128 * n, 128)] = new


def inner(adj, halo, full, kh, mid, u0, u1, u2, u3, cc, cx, cy):
    cells_x, cells_y, cols = adj.shape
    tiles, lanes = cells_y // 8 + 1, cols // 128

    @pl.loop(0, cells_x)
    def _(i):
        put(u0, i, adj[i].astype(F32), halo[i].astype(F32))

    for dst, n in ((cx, 0), (cy, 1)):
        own, side = full[:, 128 * n : 128 * n + 128].T, kh[:, 128 * n : 128 * n + 128].T
        for r in range(cells_x):
            put_coef(dst, r, own[:, r : r + 1], side[:8, r : r + 1])

    @pl.loop(1, cells_x - 1)
    def _(r):
        rest_of(cc, r, (cx, r - 1), (cx, r), (cy, r), tiles)

    levels = (u0, u1, u2, u3)
    for step in range(STEPS):
        src = levels[step]

        @pl.loop(1 + step, cells_x - 1 - step)
        def _(r, src=src, step=step):
            rows = (src, r - 1), (src, r), (src, r + 1)
            refs = (cc, r), (cx, r - 1), (cx, r), (cy, r)
            if step == STEPS - 1:
                last_row(*rows, refs, mid, r - 4, tiles, lanes)
            else:
                step_row(*rows, refs, levels[step + 1], r, tiles, lanes)


def side_rows(below, got, levels, coefs, held, lx, ly, lc, out):
    cc, cx, cy = coefs
    lanes, cells_x, depth, _ = levels[0].shape
    tiles = depth // 8 - 2
    cells_y = 8 * (tiles - 1)
    tail = 4 * cells_y + 32
    at = lambda k: cells_x - 1 - k if below else k
    sent = lambda k: -1 - k if below else k + 4
    for k in range(-4, 0):
        i = sent(k)
        own = got[cells_y * i : cells_y * (i + 1), :].astype(F32)
        side = got[4 * cells_y + 8 * i : 4 * cells_y + 8 * i + 8, :].astype(F32)
        put(held[0], k + 4, own, side)
    tile_o = got[tail : tail + 8, :].astype(F32)
    tile_h = got[tail + 8 : tail + 16, :].astype(F32)
    for dst, n in ((lx, 0), (ly, 2)):
        both = [t[:, 128 * n : 128 * n + 128] + t[:, 128 * n + 128 : 128 * n + 256] for t in (tile_o, tile_h)]
        own, side = both[0].T, both[1].T
        for k in range(-4, 0):
            r = sent(k) if below else sent(k) + 4
            put_coef(dst, k + 4, own[:, r : r + 1], side[:8, r : r + 1])

    def row(level, k):
        return (held[level], k + 4 - level) if k < level else (levels[level], at(k))

    def edge(k):
        if below:
            return (cx, at(k)) if k >= 0 else (lx, k + 4)
        return (cx, at(k) - 1) if k >= 1 else (lx, k + 3)

    def cond_y(k):
        return (cy, at(k)) if k >= 0 else (ly, k + 4)

    for k in range(-3, 1):
        rest_of(lc, k + 3, edge(k), edge(k + 1), cond_y(k), tiles)
    for level in range(STEPS):
        for k in range(level - 3, level + 1):
            rows = row(level, k - 1), row(level, k), row(level, k + 1)
            rest = (cc, at(k)) if k >= 1 else (lc, k + 3)
            refs = rest, edge(k), edge(k + 1), cond_y(k)
            if level == STEPS - 1:
                last_row(*rows, refs, out, 3 - k if below else k, tiles, lanes)
            else:
                step_row(*rows, refs, held[level + 1], k + 3 - level, tiles, lanes)


def first_side(got, u0, u1, u2, u3, cc, cx, cy, weights, mid, out, acc, h0, h1, h2, h3, lx, ly, lc):
    args = got, (u0, u1, u2, u3), (cc, cx, cy), (h0, h1, h2, h3), lx, ly, lc, out
    is_even = parity_x() == 0
    pl.when(is_even)(lambda: side_rows(True, *args))
    pl.when(jnp.logical_not(is_even))(lambda: side_rows(False, *args))
    _, cells_y, cols = mid.shape
    wide = 4 * cells_y
    base = pl.multiple_of(jnp.where(is_even, 3 * wide, 0), wide)
    acc[...] = jnp.dot(
        weights[:, wide : 3 * wide], mid[...].reshape(2 * wide, cols), preferred_element_type=F32
    ) + jnp.dot(
        weights[:, pl.ds(base, wide)], out[...].reshape(wide, cols), preferred_element_type=F32
    )


def second_side(
    got, u0, u1, u2, u3, cc, cx, cy, weights, mid, first, acc, out, send, keep,
    second, h0, h1, h2, h3, lx, ly, lc, sems,
):
    is_even = parity_x() == 0
    base_first, base_second = side_bases(u0.shape[1])
    early = [
        pltpu.make_async_copy(mid, out.at[pl.ds(4, mid.shape[0])], sems.at[0]),
        pltpu.make_async_copy(first, out.at[pl.ds(base_first, 4)], sems.at[1]),
    ]
    for copy in early:
        copy.start()
    args = got, (u0, u1, u2, u3), (cc, cx, cy), (h0, h1, h2, h3), lx, ly, lc, second
    pl.when(is_even)(lambda: side_rows(False, *args))
    pl.when(jnp.logical_not(is_even))(lambda: side_rows(True, *args))
    late = pltpu.make_async_copy(second, out.at[pl.ds(base_second, 4)], sems.at[2])
    late.start()
    _, cells_y, cols = mid.shape
    wide = 4 * cells_y
    base = pl.multiple_of(base_second * cells_y, wide)
    half = weights.shape[0] // 2
    field = second[...].reshape(wide, cols)
    for dst, rows in ((send, slice(half, 2 * half)), (keep, slice(0, half))):
        dst[...] = acc[rows, :] + jnp.dot(
            weights[rows, pl.ds(base, wide)], field, preferred_element_type=F32
        )
    for copy in early + [late]:
        copy.wait()


def pairs_even(peers):
    return [(i, i ^ 1) for i in range(peers)]


def pairs_odd(peers):
    ups = [(i, i + 1) for i in range(1, peers - 1, 2)]
    return ups + [(j, i) for i, j in ups]


def call(kernel, shapes, ins, outs, scratch, limit, flops, **more):
    return pl.pallas_call(
        kernel,
        out_shape=tuple(jax.ShapeDtypeStruct(*s) for s in shapes),
        in_specs=ins,
        out_specs=tuple(outs),
        scratch_shapes=scratch,
        compiler_params=pltpu.CompilerParams(vmem_limit_bytes=limit),
        cost_estimate=pl.CostEstimate(flops=flops, bytes_accessed=0, transcendentals=0),
        **more,
    )


def per_device(adjoint, conduct_x, conduct_y, pick_weights, owner_order):
    cells_x, cells_y, cols = adjoint.shape
    picks = pick_weights.shape[0]
    peers_x, peers_y = lax.axis_size(ALONG), lax.axis_size("gy")
    rows = 4 * cells_y + 32 + 16
    strip = ((80, cols), BF)
    payload = ((rows, cols), BF)
    dma = pltpu.SemaphoreType.DMA

    y_even, y_odd, pair, full = call(
        pack_columns,
        [strip, strip, ((cells_x, 4 * cells_y), BF), ((cells_x, 2 * cells_y), F32)],
        [HBM, HBM, HBM],
        [VMEM] * 4,
        [pltpu.VMEM((cells_x, 8, cols), BF)] * 2 + [pltpu.VMEM((cells_x, cells_y), F32)] * 2 + [dma((4,))],
        59 * MIB,
        1 << 20,
    )(adjoint, conduct_x, conduct_y)
    y_odd = lax.ppermute(y_odd, "gy", pairs_odd(peers_y))
    y_even = lax.ppermute(y_even, "gy", pairs_even(peers_y))

    weights, ready = call(
        order_weights,
        [((picks, cells_x * cells_y), BF), ((8, 128), F32)],
        [SMEM, VMEM],
        [VMEM] * 2,
        [pltpu.VMEM((cells_x * PITCH, cells_y), F32)],
        8 * MIB,
        1 << 27,
    )(owner_order, pick_weights)

    x_even, x_odd, halo, kh = call(
        pack_rows,
        [payload, payload, ((cells_x, 8, cols), BF), ((cells_x, 256), F32)],
        [HBM, VMEM, VMEM, VMEM, VMEM],
        [VMEM] * 4,
        [dma((8,))],
        8 * MIB,
        1 << 20,
    )(adjoint, pair, y_even, y_odd, ready)
    x_odd = lax.ppermute(x_odd, ALONG, pairs_odd(peers_x))
    x_even = lax.ppermute(x_even, ALONG, pairs_even(peers_x))

    depth = cells_y + 24
    level = ((cols // 128, cells_x, depth, 128), F32)
    wide = ((cells_x, depth, 128), F32)
    mid, *state = call(
        inner,
        [((8, cells_y, cols), BF)] + [level] * 4 + [wide] * 3,
        [VMEM] * 4,
        [VMEM] * 8,
        [],
        8 * MIB,
        1 << 28,
    )(adjoint, halo, full, kh)
    side = [pltpu.VMEM((cols // 128, 4, depth, 128), F32)] * 4 + [pltpu.VMEM((4, depth, 128), F32)] * 3
    edge = ((4, cells_y, cols), BF)
    first, acc = call(
        first_side,
        [edge, ((picks, cols), F32)],
        [VMEM] * 10,
        [VMEM] * 2,
        side,
        16 * MIB,
        1 << 27,
    )(x_even, *state, weights, mid)
    smoothed, send, keep = call(
        second_side,
        [(adjoint.shape, BF), ((picks // 2, cols), F32), ((picks // 2, cols), F32)],
        [VMEM] * 12,
        [HBM, VMEM, VMEM],
        [pltpu.VMEM(*edge)] + side + [dma((3,))],
        16 * MIB,
        1 << 27,
    )(x_odd, *state, weights, mid, first, acc)
    other = lax.ppermute(send, "core", [(0, 1), (1, 0)])
    merged = (keep + other).astype(BF).reshape(-1, 2, cols)
    arrived = lax.all_to_all(merged, ("g", "gy"), split_axis=0, concat_axis=0, tiled=True)
    return smoothed, arrived.astype(F32).sum(axis=0)


def solution(mesh):
    peers_x, peers_y = mesh.devices.shape
    split = Mesh(mesh.devices.reshape(peers_x // 2, 2, peers_y), ("g", "core", "gy"))
    return jax.shard_map(
        per_device,
        mesh=split,
        in_specs=(P(ALONG, "gy", None), P(ALONG, "gy"), P(ALONG, "gy"), P(None, ALONG, "gy"), P()),
        out_specs=(P(ALONG, "gy", None), P(("g", "core", "gy"), None)),
        check_vma=False,
    )
```

time: 153 us -> 63.4 us (0.41)
  starting transfers between devices: 68.1 us -> 9.06 us
  waiting for transfers between devices: 35.2 us -> 1.91 us
  blocking collectives: 0 us -> 30.9 us
  other arithmetic: 27.5 us -> 0.96 us
  Pallas kernels: 0 us -> 17.2 us
  local copies, waits for them, and re-layouts: 16.8 us -> 1.71 us
  matrix products: 3.09 us -> 0 us
    all_to_all x0 -> x1, blocking collectives: none -> 30.9 us  [per_device(): lax.all_to_all(merged, ('g', 'gy'), split_axis=0, concat_axis=0, tiled=True)]
    all_to_all x4 -> x0, starting transfers between devices: 30.7 us -> none  [summed_on_arrival(): lax.all_to_all(parts, axis, split_axis=0, concat_axis=0, tiled=True)]
    all_to_all x4 -> x0, waiting for transfers between devices: 30 us -> none  [summed_on_arrival(): lax.all_to_all(parts, axis, split_axis=0, concat_axis=0, tiled=True)]
    ppermute x12 -> x5, starting transfers between devices: 37.4 us -> 9.06 us  [the longest x1 3.65 us: per_device(): y_even = lax.ppermute(y_even, 'gy', pairs_even(peers_y))]
    pallas_call x0 -> x6, Pallas kernels: none -> 17.2 us  [the longest x1 5.39 us: per_device(): call(inner, [((8, cells_y, cols), BF)] + [level] * 4 + [wide] * 3, [VMEM]...]
    add x3 -> x0, other arithmetic: 13.5 us -> none  [diffuse(): result = result + cony[1:-1, 1:-1, None] * (rightside - centre)]
    slice x11 -> x0, local copies, waits for them, and re-layouts: 6.05 us -> none  [the longest x2 2.16 us: extended(): last = lax.slice_in_dim(array, length - width, length, axis=dim)]
    select_n x1 -> x0, local copies, waits for them, and re-layouts: 4.41 us -> none  [per_device(): jnp.take(pick_weights.reshape(picks, cells_x * cells_y), owner_order, axi...]
  transfers between devices with their start and end apart: 16 -> 5, of which waited for: 5 -> 1; matrix products, arithmetic and copies ran while one was open for 17% -> 0% of each run, Pallas kernels for 0% -> 17%
where the time goes in v1:
time: 63.4 us; the launch traced here: 62.6 us
  blocking collectives  30.9 us (49%)
  Pallas kernels  17.2 us (27%)
  starting transfers between devices  9.06 us (14%)
  waiting for transfers between devices  1.91 us (3%)
  local copies, waits for them, and re-layouts  1.71 us (3%)
  other arithmetic  0.96 us (2%)
  between operations  0.8 us (1%)
    all_to_all x1, blocking collectives, per_device(): lax.all_to_all(merged, ('g', 'gy'), split_axis=0, concat_axis=0, tiled=True)  30.9 us
    pallas_call x1, Pallas kernels, per_device(): call(inner, [((8, cells_y, cols), BF)] + [level] * 4 + [wide] * 3, [VMEM]...  5.39 us
    ppermute x1, starting transfers between devices, per_device(): y_even = lax.ppermute(y_even, 'gy', pairs_even(peers_y))  3.65 us
    pallas_call x1, Pallas kernels, per_device(): call(second_side, [(adjoint.shape, BF), ((picks // 2, cols), F32), ((pick...  3.23 us
    pallas_call x1, Pallas kernels, per_device(): call(first_side, [edge, ((picks, cols), F32)], [VMEM] * 10, [VMEM] * 2, s...  3.08 us
    ppermute x1, starting transfers between devices, per_device(): x_odd = lax.ppermute(x_odd, ALONG, pairs_odd(peers_x))  3.01 us
    pallas_call x1, Pallas kernels, per_device(): call(order_weights, [((picks, cells_x * cells_y), BF), ((8, 128), F32)],...  2.1 us
    pallas_call x1, Pallas kernels, per_device(): call(pack_columns, [strip, strip, ((cells_x, 4 * cells_y), BF), ((cells_x...  1.9 us
  transfers between devices with their start and end apart: 5, of which 1 were waited for; matrix products, arithmetic and copies ran while one was open for 0% of the time, Pallas kernels for 17%

profile of v1, /device:TPU:1, one launch (start us, length us, event | category | flops | bytes accessed | tf_op | source)
XLA Modules:
  0.0 62.6 jit_solution(15571437483185563291)
XLA Ops:
  0.6 0.0 copy-start
  0.7 1.9 %shard_map.68 = (bf16[80,512]{1,0:T(8,128)(2,1)}, bf16[80,512]{1,0:T(8,128)(2,1)}, bf16[16,512]{1,0:T(8,128)(2,1)}, f32[16,256]{1,0:T(8,128)}) custom-call(bf16[16,128,512]{2,1,0:T(8,128)(2,1)} %adj.5, f32[16,128]{1,0:T(8,128)} %kx.1, f32[16,128]{1,0:T(8,128)} %ky.1), custom_call_target="tpu_custom_call" | custom-call | flops 1048576 | tf_op jit(solution)/shard_map/pallas_call | solution.py:366
  2.6 3.6 %collective-permute-start = (bf16[80,512]{1,0:T(8,128)(2,1)}, bf16[80,512]{1,0:T(8,128)(2,1)S(1)}, u32[]{:S(2)}, u32[]{:S(2)}) collective-permute-start(bf16[80,512]{1,0:T(8,128)(2,1)} %get-tuple-element.26), channel_id=1, source_target_pairs={{0,1},{1,0},{2,3},{3,2},{4,5},{5,4},{6,7},{7,6},{8,9},{9,8},{10,11... | collective-permute-start | bytes 245768 | tf_op jit(solution)/shard_map/ppermute | solution.py:376
  6.2 0.7 %collective-permute-start.1 = (bf16[80,512]{1,0:T(8,128)(2,1)}, bf16[80,512]{1,0:T(8,128)(2,1)S(1)}, u32[]{:S(2)}, u32[]{:S(2)}) collective-permute-start(bf16[80,512]{1,0:T(8,128)(2,1)} %get-tuple-element.27), channel_id=1, source_target_pairs={{1,2},{3,4},{5,6},{2,1},{4,3},{6,5},{9,10},{11,12},{13,14},{10,9},... | collective-permute-start | bytes 245768 | tf_op jit(solution)/shard_map/ppermute | solution.py:375
  6.9 0.0 copy-done.4
  6.9 0.0 copy-start.1
  6.9 1.6 %copy-done.1 = bf16[512,16,128]{2,1,0:T(8,128)(2,1)S(1)} copy-done((bf16[512,16,128]{2,1,0:T(8,128)(2,1)S(1)}, bf16[512,16,128]{2,1,0:T(8,128)(2,1)}, u32[]{:S(2)}) %copy-start.1) | copy-done | bytes 2097176
  8.5 2.1 %shard_map.69 = (bf16[512,2048]{1,0:T(8,128)(2,1)S(1)}, f32[8,128]{1,0:T(8,128)S(1)}) custom-call(s32[512]{0:T(512)S(1)} %copy-done.4, bf16[512,16,128]{2,1,0:T(8,128)(2,1)S(1)} %copy-done.1), custom_call_target="tpu_custom_call" | custom-call | flops 134217728 | tf_op jit(solution)/shard_map/pallas_call | solution.py:378
  10.6 0.0 collective-permute-done.y_even
  10.6 0.0 collective-permute-done.1.y_odd
  10.6 1.5 %shard_map.70 = (bf16[560,512]{1,0:T(8,128)(2,1)S(1)}, bf16[560,512]{1,0:T(8,128)(2,1)S(1)}, bf16[16,8,512]{2,1,0:T(8,128)(2,1)S(1)}, f32[16,256]{1,0:T(8,128)S(1)}) custom-call(bf16[16,128,512]{2,1,0:T(8,128)(2,1)S(1)} %copy-done, bf16[16,512]{1,0:T(8,128)(2,1)S(1)} %copy-done.3, bf16[80,512]{1,0:T(8,128)(2,1)S(1)} %collective-permute-done.y_even, ...), custom_call_target="tpu_custom_call" | custom-call | flops 1048576 | tf_op jit(solution)/shard_map/pallas_call | solution.py:388
  12.2 1.5 %collective-permute-start.3 = (bf16[560,512]{1,0:T(8,128)(2,1)S(1)}, bf16[560,512]{1,0:T(8,128)(2,1)S(1)}, u32[]{:S(2)}, u32[]{:S(2)}) collective-permute-start(bf16[560,512]{1,0:T(8,128)(2,1)S(1)} %get-tuple-element.42), channel_id=1, source_target_pairs={{0,8},{8,0},{16,24},{24,16},{32,40},{40,32},{48,56},{56,48},{64,72... | collective-permute-start | bytes 1720328 | tf_op jit(solution)/shard_map/ppermute | solution.py:398
  13.7 3.0 %collective-permute-start.2 = (bf16[560,512]{1,0:T(8,128)(2,1)S(1)}, bf16[560,512]{1,0:T(8,128)(2,1)S(1)}, u32[]{:S(2)}, u32[]{:S(2)}) collective-permute-start(bf16[560,512]{1,0:T(8,128)(2,1)S(1)} %get-tuple-element.29), channel_id=1, source_target_pairs={{8,16},{24,32},{40,48},{56,64},{72,80},{88,96},{104,112},{120,128}... | collective-permute-start | bytes 1720328 | tf_op jit(solution)/shard_map/ppermute | solution.py:397
  16.7 5.4 %shard_map.71 = (bf16[8,128,512]{2,1,0:T(8,128)(2,1)S(1)}, f32[4,16,152,128]{3,2,1,0:T(8,128)S(1)}, f32[4,16,152,128]{3,2,1,0:T(8,128)S(1)}, f32[4,16,152,128]{3...) custom-call(bf16[16,128,512]{2,1,0:T(8,128)(2,1)S(1)} %copy-done, ...), custom_call_target="tpu_custom_call" | custom-call | flops 268435456 | tf_op jit(solution)/shard_map/pallas_call | solution.py:403
  22.1 0.0 collective-permute-done.3.got
  22.1 3.1 %shard_map.72 = (bf16[4,128,512]{2,1,0:T(8,128)(2,1)S(1)}, f32[512,512]{1,0:T(8,128)S(1)}) custom-call(bf16[560,512]{1,0:T(8,128)(2,1)S(1)} %collective-permute-done.3.got, f32[4,16,152,128]{3,2,1,0:T(8,128)S(1)} %get-tuple-element.33.u0, f32[4,16,152,128]{3,2,1,0:T(8,128)S(1)} %get-tuple-element.34.u1, f32[4,16,152,128]{3,2,1,0:T(8,128)S(1)} %get-tuple-element.35.u2, ...), custom_call_target="tpu_custom_call" | custom-call | flops 134217728 | tf_op jit(solution)/shard_map/pallas_call | solution.py:414
  25.2 0.0 collective-permute-done.2.got
  25.2 3.2 %shard_map.73 = (bf16[16,128,512]{2,1,0:T(8,128)(2,1)}, f32[256,512]{1,0:T(8,128)S(1)}, f32[256,512]{1,0:T(8,128)S(1)}) custom-call(bf16[560,512]{1,0:T(8,128)(2,1)S(1)} %collective-permute-done.2.got, f32[4,16,152,128]{3,2,1,0:T(8,128)S(1)} %get-tuple-element.33.u0, f32[4,16,152,128]{3,2,1,0:T(8,128)S(1)} %get-tuple-element.34.u1, ...), custom_call_target="tpu_custom_call" | custom-call | flops 134217728 | tf_op jit(solution)/shard_map/pallas_call | solution.py:423
  28.4 0.3 collective-permute-start.4
  28.7 1.9 %collective-permute-done.4 = f32[256,512]{1,0:T(8,128)S(1)} collective-permute-done((f32[256,512]{1,0:T(8,128)S(1)}, f32[256,512]{1,0:T(8,128)S(1)}, u32[]{:S(2)}, u32[]{:S(2)}) %collective-permute-start.4) | collective-permute-done | bytes 524320 | tf_op jit(solution)/shard_map/ppermute | solution.py:432
  30.6 0.1 add_convert_fusion
  30.7 0.1 reshape.7
  30.8 30.9 %all_to_all.5 = bf16[128,2,512]{2,1,0:T(2,128)(2,1)S(1)} all-to-all(bf16[128,2,512]{2,1,0:T(2,128)(2,1)S(1)} %reshape.7), channel_id=1, replica_groups=mesh['g'=16,'core'=2,'gy'=8] {'g','gy'}, dimensions={0} | all-to-all | bytes 524288 | tf_op jit(solution)/shard_map/all_to_all | solution.py:434
  61.7 0.9 %convert_reduce_fusion = f32[2,512]{1,0:T(2,128)} fusion(bf16[128,2,512]{2,1,0:T(2,128)(2,1)S(1)} %all_to_all.5), kind=kLoop, calls=%fused_computation | loop fusion | flops 261120 | bytes 266240 | tf_op jit(solution)/shard_map/reduce_sum | solution.py:435
  (6 shorter events, 0.0 us)
Async XLA Ops:
  0.6 10.0 %copy-start = (bf16[16,128,512]{2,1,0:T(8,128)(2,1)S(1)}, bf16[16,128,512]{2,1,0:T(8,128)(2,1)}, u32[]{:S(2)}) copy-start(bf16[16,128,512]{2,1,0:T(8,128)(2,1)} %adj.5) | copy-start | bytes 6291460
  0.6 6.2 %copy-start.4 = (s32[512]{0:T(512)S(1)}, s32[512]{0:T(512)}, u32[]{:S(2)}) copy-start(s32[512]{0:T(512)} %order.1) | copy-start | bytes 6148
  2.6 8.0 %collective-permute-start = (bf16[80,512]{1,0:T(8,128)(2,1)}, bf16[80,512]{1,0:T(8,128)(2,1)S(1)}, u32[]{:S(2)}, u32[]{:S(2)}) collective-permute-start(bf16[80,512]{1,0:T(8,128)(2,1)} %get-tuple-element.26), channel_id=1, source_target_pairs={{0,1},{1,0},{2,3},{3,2},{4,5},{5,4},{6,7},{7,6},{8,9},{9,8},{10,11... | collective-permute-start | bytes 245768 | tf_op jit(solution)/shard_map/ppermute | solution.py:376
  6.2 4.4 %collective-permute-start.1 = (bf16[80,512]{1,0:T(8,128)(2,1)}, bf16[80,512]{1,0:T(8,128)(2,1)S(1)}, u32[]{:S(2)}, u32[]{:S(2)}) collective-permute-start(bf16[80,512]{1,0:T(8,128)(2,1)} %get-tuple-element.27), channel_id=1, source_target_pairs={{1,2},{3,4},{5,6},{2,1},{4,3},{6,5},{9,10},{11,12},{13,14},{10,9},... | collective-permute-start | bytes 245768 | tf_op jit(solution)/shard_map/ppermute | solution.py:375
  6.9 1.6 %copy-start.1 = (bf16[512,16,128]{2,1,0:T(8,128)(2,1)S(1)}, bf16[512,16,128]{2,1,0:T(8,128)(2,1)}, u32[]{:S(2)}) copy-start(bf16[512,16,128]{2,1,0:T(8,128)(2,1)} %weights.1) | copy-start | bytes 6291460
  8.5 2.1 %copy-start.3 = (bf16[16,512]{1,0:T(8,128)(2,1)S(1)}, bf16[16,512]{1,0:T(8,128)(2,1)}, u32[]{:S(2)}) copy-start(bf16[16,512]{1,0:T(8,128)(2,1)} %get-tuple-element.25.pair) | copy-start | bytes 49156
  8.5 8.2 %copy-start.2 = (f32[16,256]{1,0:T(8,128)S(1)}, f32[16,256]{1,0:T(8,128)}, u32[]{:S(2)}) copy-start(f32[16,256]{1,0:T(8,128)} %get-tuple-element.31.full) | copy-start | bytes 49156
  12.2 9.9 %collective-permute-start.3 = (bf16[560,512]{1,0:T(8,128)(2,1)S(1)}, bf16[560,512]{1,0:T(8,128)(2,1)S(1)}, u32[]{:S(2)}, u32[]{:S(2)}) collective-permute-start(bf16[560,512]{1,0:T(8,128)(2,1)S(1)} %get-tuple-element.42), channel_id=1, source_target_pairs={{0,8},{8,0},{16,24},{24,16},{32,40},{40,32},{48,56},{56,48},{64,72... | collective-permute-start | bytes 1720328 | tf_op jit(solution)/shard_map/ppermute | solution.py:398
  13.7 11.5 %collective-permute-start.2 = (bf16[560,512]{1,0:T(8,128)(2,1)S(1)}, bf16[560,512]{1,0:T(8,128)(2,1)S(1)}, u32[]{:S(2)}, u32[]{:S(2)}) collective-permute-start(bf16[560,512]{1,0:T(8,128)(2,1)S(1)} %get-tuple-element.29), channel_id=1, source_target_pairs={{8,16},{24,32},{40,48},{56,64},{72,80},{88,96},{104,112},{120,128}... | collective-permute-start | bytes 1720328 | tf_op jit(solution)/shard_map/ppermute | solution.py:397
  28.4 2.2 %collective-permute-start.4 = (f32[256,512]{1,0:T(8,128)S(1)}, f32[256,512]{1,0:T(8,128)S(1)}, u32[]{:S(2)}, u32[]{:S(2)}) collective-permute-start(f32[256,512]{1,0:T(8,128)S(1)} %get-tuple-element.47), channel_id=1, source_target_pairs={{0,8},{8,0},{1,9},{9,1},{2,10},{10,2},{3,11},{11,3},{4,12},{12,4},... | collective-permute-start | bytes 1572872 | tf_op jit(solution)/shard_map/ppermute | solution.py:432

commit v2 on v1

--- a/solution.py
+++ b/solution.py
@@ -12,6 +12,7 @@
 VMEM = pl.BlockSpec(memory_space=pltpu.VMEM)
 SMEM = pl.BlockSpec(memory_space=pltpu.SMEM)
 HBM = pl.BlockSpec(memory_space=pltpu.HBM)
+ANY = pl.BlockSpec(memory_space=pl.ANY)
 MIB = 1024 * 1024
 ALONG = ("g", "core")
 PITCH = 520
@@ -34,18 +35,8 @@
     return lax.broadcasted_iota(jnp.int32, shape, 0) < 4
 
 
-def pack_columns(adj, kx, ky, even, odd, pair, full, first, last, kxv, kyv, sems):
-    cells_x, cells_y, _ = adj.shape
-    coefs = [
-        pltpu.make_async_copy(kx, kxv, sems.at[2]),
-        pltpu.make_async_copy(ky, kyv, sems.at[3]),
-    ]
-    strips = [
-        pltpu.make_async_copy(adj.at[:, pl.ds(0, 8)], first, sems.at[0]),
-        pltpu.make_async_copy(adj.at[:, pl.ds(cells_y - 8, 8)], last, sems.at[1]),
-    ]
-    for copy in coefs + strips:
-        copy.start()
+def pack_columns(first, last, conduct, even, odd, pair, full):
+    _, cells_x, cells_y = conduct.shape
     is_last_x = jnp.logical_and(
         lax.axis_index("g") == lax.axis_size("g") - 1, parity_x() == 1
     )
@@ -54,18 +45,14 @@
     end_y = jnp.where(is_last_y, cells_y - 1, -1)
     row = lax.broadcasted_iota(jnp.int32, (cells_x, cells_y), 0)
     col = lax.broadcasted_iota(jnp.int32, (cells_x, cells_y), 1)
-    for copy in coefs:
-        copy.wait()
-    conx = jnp.where(row == end_x, 0.0, kxv[...])
-    cony = jnp.where(col == end_y, 0.0, kyv[...])
+    conx = jnp.where(row == end_x, 0.0, conduct[0])
+    cony = jnp.where(col == end_y, 0.0, conduct[1])
     full[:, :cells_y] = conx
     full[:, cells_y:] = cony
     pieces = jnp.concatenate([*split_pair(conx), *split_pair(cony)], axis=1)
     pair[...] = pieces
     even[64:80, :] = pieces
     odd[64:80, :] = pieces
-    for copy in strips:
-        copy.wait()
     is_even = parity_y() == 0
     for i in range(8):
         a, b = first[i].astype(F32), first[i + 8].astype(F32)
@@ -82,10 +69,12 @@
     return jnp.where(is_even, cells_x - 4, 0), jnp.where(is_even, 0, cells_x - 4)
 
 
-def order_weights(order, weights, out, ready, spread):
+def order_weights(order, weights, adj, out, even, odd, spread):
     picks, cells_x, cells_y = weights.shape
     core = parity_x()
-    ready[...] = jnp.zeros_like(ready)
+    for k in range(4):
+        for base, dst in zip(side_bases(cells_x), (even, odd)):
+            dst[k * cells_y : (k + 1) * cells_y, :] = adj[base + k]
 
     @pl.loop(0, picks // 32)
     def _(g):
@@ -101,21 +90,11 @@
         out[:, pl.ds(pl.multiple_of(i * cells_y, cells_y), cells_y)] = block.astype(BF)
 
 
-def pack_rows(adj, pair, y_even, y_odd, ready, even, odd, halo, kh, sems):
-    cells_x, cells_y, _ = adj.shape
-    del ready
+def pack_rows(even_in, odd_in, pair, y_even, y_odd, even, odd, halo, kh, tail_even, tail_odd, sems):
+    del even_in, odd_in
+    cells_x = halo.shape[0]
     is_even = parity_x() == 0
     base_even, base_odd = side_bases(cells_x)
-    copies = []
-    for k in range(4):
-        for n, (base, out) in enumerate(((base_even, even), (base_odd, odd))):
-            copies.append(
-                pltpu.make_async_copy(
-                    adj.at[base + k], out.at[pl.ds(k * cells_y, cells_y)], sems.at[2 * k + n]
-                )
-            )
-    for copy in copies:
-        copy.start()
     y_is_even = parity_y() == 0
     for i in range(8):
         e, o = y_even[8 * i : 8 * i + 8, :].astype(F32), y_odd[8 * i : 8 * i + 8, :].astype(F32)
@@ -134,12 +113,17 @@
     kh[:, 128:] = parts[2] + parts[3]
     side = jnp.concatenate(parts, axis=1)
     own = pair[...].astype(F32)
-    tail = 4 * cells_y + 32
-    for base, out, flag in ((base_even, even, is_even), (base_odd, odd, jnp.logical_not(is_even))):
+    is_odd = jnp.logical_not(is_even)
+    copies = []
+    for n, (base, out, tail, flag) in enumerate(
+        ((base_even, even, tail_even, is_even), (base_odd, odd, tail_odd, is_odd))
+    ):
         for k in range(4):
-            out[4 * cells_y + 8 * k : 4 * cells_y + 8 * k + 8, :] = halo[base + k]
-        out[tail : tail + 8, :] = jnp.where(flag, own[8:], own[:8]).astype(BF)
-        out[tail + 8 : tail + 16, :] = jnp.where(flag, side[8:], side[:8]).astype(BF)
+            tail[8 * k : 8 * k + 8, :] = halo[base + k]
+        tail[32:40, :] = jnp.where(flag, own[8:], own[:8]).astype(BF)
+        tail[40:48, :] = jnp.where(flag, side[8:], side[:8]).astype(BF)
+        copies.append(pltpu.make_async_copy(tail, out.at[pl.ds(out.shape[0] - 48, 48)], sems.at[n]))
+        copies[-1].start()
     for copy in copies:
         copy.wait()
 
@@ -214,13 +198,13 @@
     cells_x, cells_y, cols = adj.shape
     tiles, lanes = cells_y // 8 + 1, cols // 128
 
-    @pl.loop(0, cells_x)
-    def _(i):
-        put(u0, i, adj[i].astype(F32), halo[i].astype(F32))
-
-    for dst, n in ((cx, 0), (cy, 1)):
-        own, side = full[:, 128 * n : 128 * n + 128].T, kh[:, 128 * n : 128 * n + 128].T
-        for r in range(cells_x):
+    turned = [
+        (dst, full[:, 128 * n : 128 * n + 128].T, kh[:, 128 * n : 128 * n + 128].T)
+        for n, dst in enumerate((cx, cy))
+    ]
+    for r in range(cells_x):
+        put(u0, r, adj[r].astype(F32), halo[r].astype(F32))
+        for dst, own, side in turned:
             put_coef(dst, r, own[:, r : r + 1], side[:8, r : r + 1])
 
     @pl.loop(1, cells_x - 1)
@@ -303,32 +287,37 @@
 
 
 def second_side(
-    got, u0, u1, u2, u3, cc, cx, cy, weights, mid, first, acc, out, send, keep,
-    second, h0, h1, h2, h3, lx, ly, lc, sems,
+    got, u0, u1, u2, u3, cc, cx, cy, weights, acc, out, send, h0, h1, h2, h3, lx, ly, lc
 ):
     is_even = parity_x() == 0
-    base_first, base_second = side_bases(u0.shape[1])
-    early = [
+    args = got, (u0, u1, u2, u3), (cc, cx, cy), (h0, h1, h2, h3), lx, ly, lc, out
+    pl.when(is_even)(lambda: side_rows(False, *args))
+    pl.when(jnp.logical_not(is_even))(lambda: side_rows(True, *args))
+    add_side(slice(weights.shape[0] // 2, weights.shape[0]), out, weights, acc, send)
+
+
+def add_side(rows, side, weights, acc, dst):
+    _, cells_y, cols = side.shape
+    wide = 4 * cells_y
+    _, base = side_bases(weights.shape[1] // cells_y)
+    dst[...] = acc[rows, :] + jnp.dot(
+        weights[rows, pl.ds(pl.multiple_of(base * cells_y, wide), wide)],
+        side[...].reshape(wide, cols),
+        preferred_element_type=F32,
+    )
+
+
+def finish(first, mid, second, weights, acc, out, keep, sems):
+    base_first, base_second = side_bases(out.shape[0])
+    copies = [
         pltpu.make_async_copy(mid, out.at[pl.ds(4, mid.shape[0])], sems.at[0]),
         pltpu.make_async_copy(first, out.at[pl.ds(base_first, 4)], sems.at[1]),
+        pltpu.make_async_copy(second, out.at[pl.ds(base_second, 4)], sems.at[2]),
     ]
-    for copy in early:
+    for copy in copies:
         copy.start()
-    args = got, (u0, u1, u2, u3), (cc, cx, cy), (h0, h1, h2, h3), lx, ly, lc, second
-    pl.when(is_even)(lambda: side_rows(False, *args))
-    pl.when(jnp.logical_not(is_even))(lambda: side_rows(True, *args))
-    late = pltpu.make_async_copy(second, out.at[pl.ds(base_second, 4)], sems.at[2])
-    late.start()
-    _, cells_y, cols = mid.shape
-    wide = 4 * cells_y
-    base = pl.multiple_of(base_second * cells_y, wide)
-    half = weights.shape[0] // 2
-    field = second[...].reshape(wide, cols)
-    for dst, rows in ((send, slice(half, 2 * half)), (keep, slice(0, half))):
-        dst[...] = acc[rows, :] + jnp.dot(
-            weights[rows, pl.ds(base, wide)], field, preferred_element_type=F32
-        )
-    for copy in early + [late]:
+    add_side(slice(0, weights.shape[0] // 2), second, weights, acc, keep)
+    for copy in copies:
         copy.wait()
 
 
@@ -366,34 +355,35 @@
     y_even, y_odd, pair, full = call(
         pack_columns,
         [strip, strip, ((cells_x, 4 * cells_y), BF), ((cells_x, 2 * cells_y), F32)],
-        [HBM, HBM, HBM],
+        [VMEM] * 3,
         [VMEM] * 4,
-        [pltpu.VMEM((cells_x, 8, cols), BF)] * 2 + [pltpu.VMEM((cells_x, cells_y), F32)] * 2 + [dma((4,))],
-        59 * MIB,
-        1 << 20,
-    )(adjoint, conduct_x, conduct_y)
+        [],
+        4 * MIB,
+        1 << 33,
+    )(adjoint[:, :8], adjoint[:, cells_y - 8 :], jnp.stack([conduct_x, conduct_y]))
     y_odd = lax.ppermute(y_odd, "gy", pairs_odd(peers_y))
     y_even = lax.ppermute(y_even, "gy", pairs_even(peers_y))
 
-    weights, ready = call(
+    weights, x_even, x_odd = call(
         order_weights,
-        [((picks, cells_x * cells_y), BF), ((8, 128), F32)],
-        [SMEM, VMEM],
-        [VMEM] * 2,
+        [((picks, cells_x * cells_y), BF), payload, payload],
+        [SMEM, VMEM, VMEM],
+        [VMEM] * 3,
         [pltpu.VMEM((cells_x * PITCH, cells_y), F32)],
         8 * MIB,
         1 << 27,
-    )(owner_order, pick_weights)
+    )(owner_order, pick_weights, adjoint)
 
     x_even, x_odd, halo, kh = call(
         pack_rows,
         [payload, payload, ((cells_x, 8, cols), BF), ((cells_x, 256), F32)],
-        [HBM, VMEM, VMEM, VMEM, VMEM],
-        [VMEM] * 4,
-        [dma((8,))],
-        8 * MIB,
+        [ANY, ANY, VMEM, VMEM, VMEM],
+        [ANY, ANY, VMEM, VMEM],
+        [pltpu.VMEM((48, cols), BF)] * 2 + [dma((2,))],
+        4 * MIB,
         1 << 20,
-    )(adjoint, pair, y_even, y_odd, ready)
+        input_output_aliases={0: 0, 1: 1},
+    )(x_even, x_odd, pair, y_even, y_odd)
     x_odd = lax.ppermute(x_odd, ALONG, pairs_odd(peers_x))
     x_even = lax.ppermute(x_even, ALONG, pairs_even(peers_x))
 
@@ -420,16 +410,25 @@
         16 * MIB,
         1 << 27,
     )(x_even, *state, weights, mid)
-    smoothed, send, keep = call(
+    second, send = call(
         second_side,
-        [(adjoint.shape, BF), ((picks // 2, cols), F32), ((picks // 2, cols), F32)],
-        [VMEM] * 12,
-        [HBM, VMEM, VMEM],
-        [pltpu.VMEM(*edge)] + side + [dma((3,))],
+        [edge, ((picks // 2, cols), F32)],
+        [VMEM] * 10,
+        [VMEM] * 2,
+        side,
         16 * MIB,
         1 << 27,
-    )(x_odd, *state, weights, mid, first, acc)
+    )(x_odd, *state, weights, acc)
     other = lax.ppermute(send, "core", [(0, 1), (1, 0)])
+    smoothed, keep = call(
+        finish,
+        [(adjoint.shape, BF), ((picks // 2, cols), F32)],
+        [VMEM] * 5,
+        [HBM, VMEM],
+        [dma((3,))],
+        8 * MIB,
+        1 << 27,
+    )(first, mid, second, weights, acc)
     merged = (keep + other).astype(BF).reshape(-1, 2, cols)
     arrived = lax.all_to_all(merged, ("g", "gy"), split_axis=0, concat_axis=0, tiled=True)
     return smoothed, arrived.astype(F32).sum(axis=0)

time: 63.4 us -> 60.9 us (0.961)
  Pallas kernels: 17.2 us -> 14.6 us
  other arithmetic: 0.96 us -> 1.67 us
  waiting for transfers between devices: 1.91 us -> 1.25 us
    pallas_call x1, Pallas kernels: 1.9 us -> 0.05 us  [per_device(): call(pack_columns, [strip, strip, ((cells_x, 4 * cells_y), BF), ((cells_x...]
    unnamed x10 -> x6, local copies, waits for them, and re-layouts: 1.6 us -> 0.01 us
    ppermute x1, waiting for transfers between devices: 1.9 us -> 0.53 us  [per_device(): other = lax.ppermute(send, 'core', [(0, 1), (1, 0)])]
    pallas_call x1, Pallas kernels: 1.55 us -> 0.22 us  [per_device(): call(pack_rows, [payload, payload, ((cells_x, 8, cols), BF), ((cells_x, 2...]
    ppermute x1, starting transfers between devices: 1.48 us -> 2.78 us  [per_device(): x_even = lax.ppermute(x_even, ALONG, pairs_even(peers_x))]
    ppermute x1, starting transfers between devices: 3.01 us -> 1.91 us  [per_device(): x_odd = lax.ppermute(x_odd, ALONG, pairs_odd(peers_x))]
    slice x0 -> x1, local copies, waits for them, and re-layouts: none -> 0.99 us  [per_device(): adjoint[:, cells_y - 8:]]
    another operation x0 -> x1, other arithmetic: none -> 0.72 us  [per_device(): jnp.stack([conduct_x, conduct_y])]
  transfers between devices with their start and end apart: 5 -> 5, of which waited for: 1 -> 2; matrix products, arithmetic and copies ran while one was open for 0% -> 0% of each run, Pallas kernels for 17% -> 20%
where the time goes in v2:
time: 60.9 us; the launch traced here: 60.1 us
  blocking collectives  31.5 us (52%)
  Pallas kernels  14.6 us (24%)
  starting transfers between devices  9.26 us (15%)
  other arithmetic  1.67 us (3%)
  waiting for transfers between devices  1.25 us (2%)
  local copies, waits for them, and re-layouts  1.11 us (2%)
  between operations  0.76 us (1%)
    all_to_all x1, blocking collectives, per_device(): lax.all_to_all(merged, ('g', 'gy'), split_axis=0, concat_axis=0, tiled=True)  31.5 us
    pallas_call x1, Pallas kernels, per_device(): call(inner, [((8, cells_y, cols), BF)] + [level] * 4 + [wide] * 3, [VMEM]...  5.29 us
    ppermute x1, starting transfers between devices, per_device(): y_even = lax.ppermute(y_even, 'gy', pairs_even(peers_y))  3.65 us
    pallas_call x1, Pallas kernels, per_device(): call(first_side, [edge, ((picks, cols), F32)], [VMEM] * 10, [VMEM] * 2, s...  3.08 us
    ppermute x1, starting transfers between devices, per_device(): x_even = lax.ppermute(x_even, ALONG, pairs_even(peers_x))  2.78 us
    pallas_call x1, Pallas kernels, per_device(): call(second_side, [edge, ((picks // 2, cols), F32)], [VMEM] * 10, [VMEM]...  2.38 us
    pallas_call x1, Pallas kernels, per_device(): call(order_weights, [((picks, cells_x * cells_y), BF), payload, payload],...  2.17 us
    ppermute x1, starting transfers between devices, per_device(): x_odd = lax.ppermute(x_odd, ALONG, pairs_odd(peers_x))  1.91 us
  transfers between devices with their start and end apart: 5, of which 2 were waited for; matrix products, arithmetic and copies ran while one was open for 0% of the time, Pallas kernels for 20%

profile of v2, /device:TPU:1, one launch (start us, length us, event | category | flops | bytes accessed | tf_op | source)
XLA Modules:
  0.0 60.1 jit_solution(10977852653788858598)
XLA Ops:
  0.6 1.0 %fusion = (bf16[16,8,512]{2,1,0:T(8,128)(2,1)S(1)}, bf16[16,8,512]{2,1,0:T(8,128)(2,1)S(1)}) fusion(bf16[16,128,512]{2,1,0:T(8,128)(2,1)} %adj.3), kind=kLoop, calls=%fused_computation.3 | loop fusion | bytes 524288 | tf_op jit(solution)/shard_map/slice | solution.py:363
  1.6 0.7 %pad_maximum_fusion.conduct = f32[2,16,128]{2,1,0:T(8,128)S(1)} fusion(f32[1,16,128]{2,1,0:T(8,128)} %bitcast.2, f32[1,16,128]{2,1,0:T(8,128)} %bitcast.3), kind=kLoop, calls=%fused_computation.2 | loop fusion | flops 4096 | bytes 32768 | tf_op jit(solution)/shard_map/stack | solution.py:363
  2.3 0.1 shard_map.69
  2.4 3.6 %collective-permute-start = (bf16[80,512]{1,0:T(8,128)(2,1)S(1)}, bf16[80,512]{1,0:T(8,128)(2,1)S(1)}, u32[]{:S(2)}, u32[]{:S(2)}) collective-permute-start(bf16[80,512]{1,0:T(8,128)(2,1)S(1)} %get-tuple-element.30), channel_id=1, source_target_pairs={{0,1},{1,0},{2,3},{3,2},{4,5},{5,4},{6,7},{7,6},{8,9},{9,8},{10,11... | collective-permute-start | bytes 245768 | tf_op jit(solution)/shard_map/ppermute | solution.py:365
  6.1 0.7 %collective-permute-start.1 = (bf16[80,512]{1,0:T(8,128)(2,1)S(1)}, bf16[80,512]{1,0:T(8,128)(2,1)S(1)}, u32[]{:S(2)}, u32[]{:S(2)}) collective-permute-start(bf16[80,512]{1,0:T(8,128)(2,1)S(1)} %get-tuple-element.31), channel_id=1, source_target_pairs={{1,2},{3,4},{5,6},{2,1},{4,3},{6,5},{9,10},{11,12},{13,14},{10,9},... | collective-permute-start | bytes 245768 | tf_op jit(solution)/shard_map/ppermute | solution.py:364
  6.7 0.0 copy-done
  6.7 2.2 %shard_map.68 = (bf16[512,2048]{1,0:T(8,128)(2,1)S(1)}, bf16[560,512]{1,0:T(8,128)(2,1)S(1)}, bf16[560,512]{1,0:T(8,128)(2,1)S(1)}) custom-call(s32[512]{0:T(512)S(1)} %copy-done.2, bf16[512,16,128]{2,1,0:T(8,128)(2,1)S(1)} %copy-done.1, bf16[16,128,512]{2,1,0:T(8,128)(2,1)S(1)} %copy-done), custom_call_target="tpu_custom_call" | custom-call | flops 134217728 | tf_op jit(solution)/shard_map/pallas_call | solution.py:367
  8.9 0.0 collective-permute-done.y_even
  8.9 0.0 collective-permute-done.1.y_odd
  8.9 0.2 shard_map.70
  9.2 2.8 %collective-permute-start.2 = (bf16[560,512]{1,0:T(8,128)(2,1)S(1)}, bf16[560,512]{1,0:T(8,128)(2,1)S(1)}, u32[]{:S(2)}, u32[]{:S(2)}) collective-permute-start(bf16[560,512]{1,0:T(8,128)(2,1)S(1)} %get-tuple-element.32), channel_id=1, source_target_pairs={{0,8},{8,0},{16,24},{24,16},{32,40},{40,32},{48,56},{56,48},{64,72... | collective-permute-start | bytes 1720328 | tf_op jit(solution)/shard_map/ppermute | solution.py:388
  12.0 1.9 %collective-permute-start.3 = (bf16[560,512]{1,0:T(8,128)(2,1)S(1)}, bf16[560,512]{1,0:T(8,128)(2,1)S(1)}, u32[]{:S(2)}, u32[]{:S(2)}) collective-permute-start(bf16[560,512]{1,0:T(8,128)(2,1)S(1)} %get-tuple-element.46), channel_id=1, source_target_pairs={{8,16},{24,32},{40,48},{56,64},{72,80},{88,96},{104,112},{120,128}... | collective-permute-start | bytes 1720328 | tf_op jit(solution)/shard_map/ppermute | solution.py:387
  13.9 5.3 %shard_map.71 = (bf16[8,128,512]{2,1,0:T(8,128)(2,1)S(1)}, f32[4,16,152,128]{3,2,1,0:T(8,128)S(1)}, f32[4,16,152,128]{3,2,1,0:T(8,128)S(1)}, f32[4,16,152,128]{3...) custom-call(bf16[16,128,512]{2,1,0:T(8,128)(2,1)S(1)} %copy-done, ...), custom_call_target="tpu_custom_call" | custom-call | flops 268435456 | tf_op jit(solution)/shard_map/pallas_call | solution.py:393
  19.2 0.0 collective-permute-done.2.got
  19.2 3.1 %shard_map.72 = (bf16[4,128,512]{2,1,0:T(8,128)(2,1)S(1)}, f32[512,512]{1,0:T(8,128)S(1)}) custom-call(bf16[560,512]{1,0:T(8,128)(2,1)S(1)} %collective-permute-done.2.got, f32[4,16,152,128]{3,2,1,0:T(8,128)S(1)} %get-tuple-element.36.u0, f32[4,16,152,128]{3,2,1,0:T(8,128)S(1)} %get-tuple-element.37.u1, f32[4,16,152,128]{3,2,1,0:T(8,128)S(1)} %get-tuple-element.38.u2, ...), custom_call_target="tpu_custom_call" | custom-call | flops 134217728 | tf_op jit(solution)/shard_map/pallas_call | solution.py:404
  22.3 0.7 %collective-permute-done.3.got = bf16[560,512]{1,0:T(8,128)(2,1)S(1)} collective-permute-done((bf16[560,512]{1,0:T(8,128)(2,1)S(1)}, bf16[560,512]{1,0:T(8,128)(2,1)S(1)}, u32[]{:S(2)}, u32[]{:S(2)}) %collective-permute-start.3) | collective-permute-done | bytes 573472 | tf_op jit(solution)/shard_map/ppermute | solution.py:387
  23.0 2.4 %shard_map.73 = (bf16[4,128,512]{2,1,0:T(8,128)(2,1)S(1)}, f32[256,512]{1,0:T(8,128)S(1)}) custom-call(bf16[560,512]{1,0:T(8,128)(2,1)S(1)} %collective-permute-done.3.got, f32[4,16,152,128]{3,2,1,0:T(8,128)S(1)} %get-tuple-element.36.u0, f32[4,16,152,128]{3,2,1,0:T(8,128)S(1)} %get-tuple-element.37.u1, f32[4,16,152,128]{3,2,1,0:T(8,128)S(1)} %get-tuple-element.38.u2, ...), custom_call_target="tpu_custom_call" | custom-call | flops 134217728 | tf_op jit(solution)/shard_map/pallas_call | solution.py:413
  25.4 0.3 collective-permute-start.4
  25.6 1.4 %shard_map.74 = (bf16[16,128,512]{2,1,0:T(8,128)(2,1)}, f32[256,512]{1,0:T(8,128)S(1)}) custom-call(bf16[4,128,512]{2,1,0:T(8,128)(2,1)S(1)} %get-tuple-element.45.first, bf16[8,128,512]{2,1,0:T(8,128)(2,1)S(1)} %get-tuple-element.44.mid, bf16[4,128,512]{2,1,0:T(8,128)(2,1)S(1)} %get-tuple-element.48.second, ...), custom_call_target="tpu_custom_call" | custom-call | flops 134217728 | tf_op jit(solution)/shard_map/pallas_call | solution.py:423
  27.0 0.5 collective-permute-done.4
  27.5 0.1 add_convert_fusion
  27.6 0.1 reshape.7
  27.7 31.5 %all_to_all.5 = bf16[128,2,512]{2,1,0:T(2,128)(2,1)S(1)} all-to-all(bf16[128,2,512]{2,1,0:T(2,128)(2,1)S(1)} %reshape.7), channel_id=1, replica_groups=mesh['g'=16,'core'=2,'gy'=8] {'g','gy'}, dimensions={0} | all-to-all | bytes 524288 | tf_op jit(solution)/shard_map/all_to_all | solution.py:433
  59.2 0.9 %convert_reduce_fusion = f32[2,512]{1,0:T(2,128)} fusion(bf16[128,2,512]{2,1,0:T(2,128)(2,1)S(1)} %all_to_all.5), kind=kLoop, calls=%fused_computation | loop fusion | flops 261120 | bytes 266240 | tf_op jit(solution)/shard_map/reduce_sum | solution.py:434
  (5 shorter events, 0.0 us)
Async XLA Ops:
  2.3 4.4 %copy-start = (bf16[16,128,512]{2,1,0:T(8,128)(2,1)S(1)}, bf16[16,128,512]{2,1,0:T(8,128)(2,1)}, u32[]{:S(2)}) copy-start(bf16[16,128,512]{2,1,0:T(8,128)(2,1)} %adj.3) | copy-start | bytes 6291460
  2.3 4.4 %copy-start.1 = (bf16[512,16,128]{2,1,0:T(8,128)(2,1)S(1)}, bf16[512,16,128]{2,1,0:T(8,128)(2,1)}, u32[]{:S(2)}) copy-start(bf16[512,16,128]{2,1,0:T(8,128)(2,1)} %weights.1) | copy-start | bytes 6291460
  2.3 4.4 %copy-start.2 = (s32[512]{0:T(512)S(1)}, s32[512]{0:T(512)}, u32[]{:S(2)}) copy-start(s32[512]{0:T(512)} %order.1) | copy-start | bytes 6148
  2.4 6.5 %collective-permute-start = (bf16[80,512]{1,0:T(8,128)(2,1)S(1)}, bf16[80,512]{1,0:T(8,128)(2,1)S(1)}, u32[]{:S(2)}, u32[]{:S(2)}) collective-permute-start(bf16[80,512]{1,0:T(8,128)(2,1)S(1)} %get-tuple-element.30), channel_id=1, source_target_pairs={{0,1},{1,0},{2,3},{3,2},{4,5},{5,4},{6,7},{7,6},{8,9},{9,8},{10,11... | collective-permute-start | bytes 245768 | tf_op jit(solution)/shard_map/ppermute | solution.py:365
  6.1 2.9 %collective-permute-start.1 = (bf16[80,512]{1,0:T(8,128)(2,1)S(1)}, bf16[80,512]{1,0:T(8,128)(2,1)S(1)}, u32[]{:S(2)}, u32[]{:S(2)}) collective-permute-start(bf16[80,512]{1,0:T(8,128)(2,1)S(1)} %get-tuple-element.31), channel_id=1, source_target_pairs={{1,2},{3,4},{5,6},{2,1},{4,3},{6,5},{9,10},{11,12},{13,14},{10,9},... | collective-permute-start | bytes 245768 | tf_op jit(solution)/shard_map/ppermute | solution.py:364
  9.2 10.0 %collective-permute-start.2 = (bf16[560,512]{1,0:T(8,128)(2,1)S(1)}, bf16[560,512]{1,0:T(8,128)(2,1)S(1)}, u32[]{:S(2)}, u32[]{:S(2)}) collective-permute-start(bf16[560,512]{1,0:T(8,128)(2,1)S(1)} %get-tuple-element.32), channel_id=1, source_target_pairs={{0,8},{8,0},{16,24},{24,16},{32,40},{40,32},{48,56},{56,48},{64,72... | collective-permute-start | bytes 1720328 | tf_op jit(solution)/shard_map/ppermute | solution.py:388
  12.0 11.0 %collective-permute-start.3 = (bf16[560,512]{1,0:T(8,128)(2,1)S(1)}, bf16[560,512]{1,0:T(8,128)(2,1)S(1)}, u32[]{:S(2)}, u32[]{:S(2)}) collective-permute-start(bf16[560,512]{1,0:T(8,128)(2,1)S(1)} %get-tuple-element.46), channel_id=1, source_target_pairs={{8,16},{24,32},{40,48},{56,64},{72,80},{88,96},{104,112},{120,128}... | collective-permute-start | bytes 1720328 | tf_op jit(solution)/shard_map/ppermute | solution.py:387
  25.4 2.2 %collective-permute-start.4 = (f32[256,512]{1,0:T(8,128)S(1)}, f32[256,512]{1,0:T(8,128)S(1)}, u32[]{:S(2)}, u32[]{:S(2)}) collective-permute-start(f32[256,512]{1,0:T(8,128)S(1)} %get-tuple-element.51), channel_id=1, source_target_pairs={{0,8},{8,0},{1,9},{9,1},{2,10},{10,2},{3,11},{11,3},{4,12},{12,4},... | collective-permute-start | bytes 1572872 | tf_op jit(solution)/shard_map/ppermute | solution.py:422

commit v3 on v2

--- a/solution.py
+++ b/solution.py
@@ -319,6 +319,15 @@
     add_side(slice(0, weights.shape[0] // 2), second, weights, acc, keep)
     for copy in copies:
         copy.wait()
+
+
+def add_up(parts, out):
+    totals = [parts[n].astype(F32) for n in range(8)]
+    for m in range(8, parts.shape[0], 8):
+        totals = [t + parts[m + n].astype(F32) for n, t in enumerate(totals)]
+    while len(totals) > 1:
+        totals = [a + b for a, b in zip(totals[::2], totals[1::2])]
+    out[...] = totals[0]
 
 
 def pairs_even(peers):
@@ -431,7 +440,10 @@
     )(first, mid, second, weights, acc)
     merged = (keep + other).astype(BF).reshape(-1, 2, cols)
     arrived = lax.all_to_all(merged, ("g", "gy"), split_axis=0, concat_axis=0, tiled=True)
-    return smoothed, arrived.astype(F32).sum(axis=0)
+    (owned,) = call(
+        add_up, [((2, cols), F32)], [VMEM], [VMEM], [], 4 * MIB, 1 << 20
+    )(arrived)
+    return smoothed, owned
 
 
 def solution(mesh):

time: 60.9 us -> 60.7 us (level)
  other arithmetic: 1.67 us -> 0.81 us
    reduce_sum x1 -> x0, other arithmetic: 0.87 us -> none  [per_device(): return (smoothed, arrived.astype(F32).sum(axis=0))]
    pallas_call x0 -> x1, Pallas kernels: none -> 0.63 us  [per_device(): call(add_up, [((2, cols), F32)], [VMEM], [VMEM], [], 4 * MIB, 1 << 20)]
where the time goes in v3:
time: 60.7 us; the launch traced here: 59.8 us
  blocking collectives  31.5 us (52%)
  Pallas kernels  15.2 us (25%)
  starting transfers between devices  9.26 us (15%)
  waiting for transfers between devices  1.25 us (2%)
  local copies, waits for them, and re-layouts  1.11 us (2%)
  other arithmetic  0.81 us (1%)
  between operations  0.76 us (1%)
    all_to_all x1, blocking collectives, per_device(): lax.all_to_all(merged, ('g', 'gy'), split_axis=0, concat_axis=0, tiled=True)  31.5 us
    pallas_call x1, Pallas kernels, per_device(): call(inner, [((8, cells_y, cols), BF)] + [level] * 4 + [wide] * 3, [VMEM]...  5.29 us
    ppermute x1, starting transfers between devices, per_device(): y_even = lax.ppermute(y_even, 'gy', pairs_even(peers_y))  3.65 us
    pallas_call x1, Pallas kernels, per_device(): call(first_side, [edge, ((picks, cols), F32)], [VMEM] * 10, [VMEM] * 2, s...  3.08 us
    ppermute x1, starting transfers between devices, per_device(): x_even = lax.ppermute(x_even, ALONG, pairs_even(peers_x))  2.78 us
    pallas_call x1, Pallas kernels, per_device(): call(second_side, [edge, ((picks // 2, cols), F32)], [VMEM] * 10, [VMEM]...  2.38 us
    pallas_call x1, Pallas kernels, per_device(): call(order_weights, [((picks, cells_x * cells_y), BF), payload, payload],...  2.17 us
    ppermute x1, starting transfers between devices, per_device(): x_odd = lax.ppermute(x_odd, ALONG, pairs_odd(peers_x))  1.91 us
  transfers between devices with their start and end apart: 5, of which 2 were waited for; matrix products, arithmetic and copies ran while one was open for 0% of the time, Pallas kernels for 20%

profile of v3, /device:TPU:1, one launch (start us, length us, event | category | flops | bytes accessed | tf_op | source)
XLA Modules:
  0.0 59.8 jit_solution(15798349706451294057)
XLA Ops:
  0.6 1.0 %fusion = (bf16[16,8,512]{2,1,0:T(8,128)(2,1)S(1)}, bf16[16,8,512]{2,1,0:T(8,128)(2,1)S(1)}) fusion(bf16[16,128,512]{2,1,0:T(8,128)(2,1)} %adj.3), kind=kLoop, calls=%fused_computation.2 | loop fusion | bytes 524288 | tf_op jit(solution)/shard_map/slice | solution.py:372
  1.6 0.7 %pad_maximum_fusion.conduct = f32[2,16,128]{2,1,0:T(8,128)S(1)} fusion(f32[1,16,128]{2,1,0:T(8,128)} %bitcast.2, f32[1,16,128]{2,1,0:T(8,128)} %bitcast.3), kind=kLoop, calls=%fused_computation.1 | loop fusion | flops 4096 | bytes 32768 | tf_op jit(solution)/shard_map/stack | solution.py:372
  2.3 0.1 shard_map.69
  2.4 3.6 %collective-permute-start = (bf16[80,512]{1,0:T(8,128)(2,1)S(1)}, bf16[80,512]{1,0:T(8,128)(2,1)S(1)}, u32[]{:S(2)}, u32[]{:S(2)}) collective-permute-start(bf16[80,512]{1,0:T(8,128)(2,1)S(1)} %get-tuple-element.30), channel_id=1, source_target_pairs={{0,1},{1,0},{2,3},{3,2},{4,5},{5,4},{6,7},{7,6},{8,9},{9,8},{10,11... | collective-permute-start | bytes 245768 | tf_op jit(solution)/shard_map/ppermute | solution.py:374
  6.1 0.7 %collective-permute-start.1 = (bf16[80,512]{1,0:T(8,128)(2,1)S(1)}, bf16[80,512]{1,0:T(8,128)(2,1)S(1)}, u32[]{:S(2)}, u32[]{:S(2)}) collective-permute-start(bf16[80,512]{1,0:T(8,128)(2,1)S(1)} %get-tuple-element.31), channel_id=1, source_target_pairs={{1,2},{3,4},{5,6},{2,1},{4,3},{6,5},{9,10},{11,12},{13,14},{10,9},... | collective-permute-start | bytes 245768 | tf_op jit(solution)/shard_map/ppermute | solution.py:373
  6.7 0.0 copy-done
  6.7 2.2 %shard_map.68 = (bf16[512,2048]{1,0:T(8,128)(2,1)S(1)}, bf16[560,512]{1,0:T(8,128)(2,1)S(1)}, bf16[560,512]{1,0:T(8,128)(2,1)S(1)}) custom-call(s32[512]{0:T(512)S(1)} %copy-done.2, bf16[512,16,128]{2,1,0:T(8,128)(2,1)S(1)} %copy-done.1, bf16[16,128,512]{2,1,0:T(8,128)(2,1)S(1)} %copy-done), custom_call_target="tpu_custom_call" | custom-call | flops 134217728 | tf_op jit(solution)/shard_map/pallas_call | solution.py:376
  8.9 0.0 collective-permute-done.y_even
  8.9 0.0 collective-permute-done.1.y_odd
  8.9 0.2 shard_map.70
  9.2 2.8 %collective-permute-start.2 = (bf16[560,512]{1,0:T(8,128)(2,1)S(1)}, bf16[560,512]{1,0:T(8,128)(2,1)S(1)}, u32[]{:S(2)}, u32[]{:S(2)}) collective-permute-start(bf16[560,512]{1,0:T(8,128)(2,1)S(1)} %get-tuple-element.32), channel_id=1, source_target_pairs={{0,8},{8,0},{16,24},{24,16},{32,40},{40,32},{48,56},{56,48},{64,72... | collective-permute-start | bytes 1720328 | tf_op jit(solution)/shard_map/ppermute | solution.py:397
  12.0 1.9 %collective-permute-start.3 = (bf16[560,512]{1,0:T(8,128)(2,1)S(1)}, bf16[560,512]{1,0:T(8,128)(2,1)S(1)}, u32[]{:S(2)}, u32[]{:S(2)}) collective-permute-start(bf16[560,512]{1,0:T(8,128)(2,1)S(1)} %get-tuple-element.46), channel_id=1, source_target_pairs={{8,16},{24,32},{40,48},{56,64},{72,80},{88,96},{104,112},{120,128}... | collective-permute-start | bytes 1720328 | tf_op jit(solution)/shard_map/ppermute | solution.py:396
  13.9 5.3 %shard_map.71 = (bf16[8,128,512]{2,1,0:T(8,128)(2,1)S(1)}, f32[4,16,152,128]{3,2,1,0:T(8,128)S(1)}, f32[4,16,152,128]{3,2,1,0:T(8,128)S(1)}, f32[4,16,152,128]{3...) custom-call(bf16[16,128,512]{2,1,0:T(8,128)(2,1)S(1)} %copy-done, ...), custom_call_target="tpu_custom_call" | custom-call | flops 268435456 | tf_op jit(solution)/shard_map/pallas_call | solution.py:402
  19.2 0.0 collective-permute-done.2.got
  19.2 3.1 %shard_map.72 = (bf16[4,128,512]{2,1,0:T(8,128)(2,1)S(1)}, f32[512,512]{1,0:T(8,128)S(1)}) custom-call(bf16[560,512]{1,0:T(8,128)(2,1)S(1)} %collective-permute-done.2.got, f32[4,16,152,128]{3,2,1,0:T(8,128)S(1)} %get-tuple-element.36.u0, f32[4,16,152,128]{3,2,1,0:T(8,128)S(1)} %get-tuple-element.37.u1, f32[4,16,152,128]{3,2,1,0:T(8,128)S(1)} %get-tuple-element.38.u2, ...), custom_call_target="tpu_custom_call" | custom-call | flops 134217728 | tf_op jit(solution)/shard_map/pallas_call | solution.py:413
  22.3 0.7 %collective-permute-done.3.got = bf16[560,512]{1,0:T(8,128)(2,1)S(1)} collective-permute-done((bf16[560,512]{1,0:T(8,128)(2,1)S(1)}, bf16[560,512]{1,0:T(8,128)(2,1)S(1)}, u32[]{:S(2)}, u32[]{:S(2)}) %collective-permute-start.3) | collective-permute-done | bytes 573472 | tf_op jit(solution)/shard_map/ppermute | solution.py:396
  23.0 2.4 %shard_map.73 = (bf16[4,128,512]{2,1,0:T(8,128)(2,1)S(1)}, f32[256,512]{1,0:T(8,128)S(1)}) custom-call(bf16[560,512]{1,0:T(8,128)(2,1)S(1)} %collective-permute-done.3.got, f32[4,16,152,128]{3,2,1,0:T(8,128)S(1)} %get-tuple-element.36.u0, f32[4,16,152,128]{3,2,1,0:T(8,128)S(1)} %get-tuple-element.37.u1, f32[4,16,152,128]{3,2,1,0:T(8,128)S(1)} %get-tuple-element.38.u2, ...), custom_call_target="tpu_custom_call" | custom-call | flops 134217728 | tf_op jit(solution)/shard_map/pallas_call | solution.py:422
  25.4 0.3 collective-permute-start.4
  25.6 1.4 %shard_map.74 = (bf16[16,128,512]{2,1,0:T(8,128)(2,1)}, f32[256,512]{1,0:T(8,128)S(1)}) custom-call(bf16[4,128,512]{2,1,0:T(8,128)(2,1)S(1)} %get-tuple-element.45.first, bf16[8,128,512]{2,1,0:T(8,128)(2,1)S(1)} %get-tuple-element.44.mid, bf16[4,128,512]{2,1,0:T(8,128)(2,1)S(1)} %get-tuple-element.48.second, ...), custom_call_target="tpu_custom_call" | custom-call | flops 134217728 | tf_op jit(solution)/shard_map/pallas_call | solution.py:432
  27.0 0.5 collective-permute-done.4
  27.5 0.1 add_convert_fusion
  27.6 0.1 reshape.7
  27.7 31.5 %all_to_all.5.parts = bf16[128,2,512]{2,1,0:T(2,128)(2,1)S(1)} all-to-all(bf16[128,2,512]{2,1,0:T(2,128)(2,1)S(1)} %reshape.7), channel_id=1, replica_groups=mesh['g'=16,'core'=2,'gy'=8] {'g','gy'}, dimensions={0} | all-to-all | bytes 524288 | tf_op jit(solution)/shard_map/all_to_all | solution.py:442
  59.2 0.6 %shard_map.75 = f32[2,512]{1,0:T(2,128)} custom-call(bf16[128,2,512]{2,1,0:T(2,128)(2,1)S(1)} %all_to_all.5.parts), custom_call_target="tpu_custom_call" | custom-call | flops 1048576 | tf_op jit(solution)/shard_map/pallas_call | solution.py:443
  (5 shorter events, 0.0 us)
Async XLA Ops:
  2.3 4.4 %copy-start = (bf16[16,128,512]{2,1,0:T(8,128)(2,1)S(1)}, bf16[16,128,512]{2,1,0:T(8,128)(2,1)}, u32[]{:S(2)}) copy-start(bf16[16,128,512]{2,1,0:T(8,128)(2,1)} %adj.3) | copy-start | bytes 6291460
  2.3 4.4 %copy-start.1 = (bf16[512,16,128]{2,1,0:T(8,128)(2,1)S(1)}, bf16[512,16,128]{2,1,0:T(8,128)(2,1)}, u32[]{:S(2)}) copy-start(bf16[512,16,128]{2,1,0:T(8,128)(2,1)} %weights.1) | copy-start | bytes 6291460
  2.3 4.4 %copy-start.2 = (s32[512]{0:T(512)S(1)}, s32[512]{0:T(512)}, u32[]{:S(2)}) copy-start(s32[512]{0:T(512)} %order.1) | copy-start | bytes 6148
  2.4 6.5 %collective-permute-start = (bf16[80,512]{1,0:T(8,128)(2,1)S(1)}, bf16[80,512]{1,0:T(8,128)(2,1)S(1)}, u32[]{:S(2)}, u32[]{:S(2)}) collective-permute-start(bf16[80,512]{1,0:T(8,128)(2,1)S(1)} %get-tuple-element.30), channel_id=1, source_target_pairs={{0,1},{1,0},{2,3},{3,2},{4,5},{5,4},{6,7},{7,6},{8,9},{9,8},{10,11... | collective-permute-start | bytes 245768 | tf_op jit(solution)/shard_map/ppermute | solution.py:374
  6.1 2.9 %collective-permute-start.1 = (bf16[80,512]{1,0:T(8,128)(2,1)S(1)}, bf16[80,512]{1,0:T(8,128)(2,1)S(1)}, u32[]{:S(2)}, u32[]{:S(2)}) collective-permute-start(bf16[80,512]{1,0:T(8,128)(2,1)S(1)} %get-tuple-element.31), channel_id=1, source_target_pairs={{1,2},{3,4},{5,6},{2,1},{4,3},{6,5},{9,10},{11,12},{13,14},{10,9},... | collective-permute-start | bytes 245768 | tf_op jit(solution)/shard_map/ppermute | solution.py:373
  9.2 10.0 %collective-permute-start.2 = (bf16[560,512]{1,0:T(8,128)(2,1)S(1)}, bf16[560,512]{1,0:T(8,128)(2,1)S(1)}, u32[]{:S(2)}, u32[]{:S(2)}) collective-permute-start(bf16[560,512]{1,0:T(8,128)(2,1)S(1)} %get-tuple-element.32), channel_id=1, source_target_pairs={{0,8},{8,0},{16,24},{24,16},{32,40},{40,32},{48,56},{56,48},{64,72... | collective-permute-start | bytes 1720328 | tf_op jit(solution)/shard_map/ppermute | solution.py:397
  12.0 11.0 %collective-permute-start.3 = (bf16[560,512]{1,0:T(8,128)(2,1)S(1)}, bf16[560,512]{1,0:T(8,128)(2,1)S(1)}, u32[]{:S(2)}, u32[]{:S(2)}) collective-permute-start(bf16[560,512]{1,0:T(8,128)(2,1)S(1)} %get-tuple-element.46), channel_id=1, source_target_pairs={{8,16},{24,32},{40,48},{56,64},{72,80},{88,96},{104,112},{120,128}... | collective-permute-start | bytes 1720328 | tf_op jit(solution)/shard_map/ppermute | solution.py:396
  25.4 2.2 %collective-permute-start.4 = (f32[256,512]{1,0:T(8,128)S(1)}, f32[256,512]{1,0:T(8,128)S(1)}, u32[]{:S(2)}, u32[]{:S(2)}) collective-permute-start(f32[256,512]{1,0:T(8,128)S(1)} %get-tuple-element.51), channel_id=1, source_target_pairs={{0,8},{8,0},{1,9},{9,1},{2,10},{10,2},{3,11},{11,3},{4,12},{12,4},... | collective-permute-start | bytes 1572872 | tf_op jit(solution)/shard_map/ppermute | solution.py:431
